TPU v7x, 32 devices: a whole 2x2x4 slice. The times are simulated.
32 devices in a mesh: ctx: 16 (over z, y, x), tp: 2 (over core).
Axes of the slice: x: 2, y: 2, z: 4, core: 2. Of those that a mesh axis runs over, the one named last changes fastest.
Arguments:
- queries: bfloat16 [1024, 2560], P('ctx', 'tp'), may hold values from -100 to 100
- projected_keys: bfloat16 [1024, 512], P('ctx', 'tp'), may hold values from -30 to 30
- projected_values: bfloat16 [1024, 512], P('ctx', 'tp'), may hold values from -6 to 6
- hidden: bfloat16 [1024, 5120], P('ctx', 'tp'), may hold values from -6 to 6
- route_ids: int32 [1024, 1], P('ctx'), may hold values from 0 to 15; in each aligned block of 64 rows (0 to 63, 64 to 127, ...) at most 6 rows name the same one
- route_gain: float32 [1024], P('ctx'), may hold values from 0.25 to 1
- w_gate: bfloat16 [16, 5120, 4096], P('ctx', None, 'tp'), may hold values from -0.078125 to 0.078125
- w_up: bfloat16 [16, 5120, 4096], P('ctx', None, 'tp'), may hold values from -0.078125 to 0.078125
- w_down: bfloat16 [16, 4096, 5120], P('ctx', None, 'tp'), may hold values from -0.09375 to 0.09375
Outputs:
- attended: bfloat16 [1024, 2560], P('ctx', 'tp')
- mixed: bfloat16 [1024, 5120], P('ctx', 'tp')
Inputs may be any that keep to these rules, and one draw needn't show every extreme that they name: `route_ids`: within the rows of one device (aligned blocks of 64 rows) no expert is named more than 6 times, a bound that some block reaches.
All inputs are finite; a program needn't handle non-finite values.
Results may differ from a plain program's by a relative error of at most 0.0057.
Values may be sent and summed in bfloat16 or wider, within the bound.
No kernel may reach another device: no remote copies, remote signals or barrier semaphores. Data moves between devices by JAX's collectives and lax.ppermute only.
A program may use at most 128 MiB of HBM per device.

v0:
```python
import math

import jax
import jax.numpy as jnp
from jax import lax
from jax.sharding import PartitionSpec as P

HEAD_SIZE = 128
EXPERTS = 16
CAP = 6


masked_score = -1e30


def body(
    queries, projected_keys, projected_values, hidden, route_ids, route_gain, w_gate, w_up, w_down
):
    tok_rows = queries.shape[0]
    width_q = queries.shape[1]
    width_kv = projected_keys.shape[1]
    ctx_count = lax.axis_size("ctx")
    ctx_index = lax.axis_index("ctx")
    offsets = jnp.arange(tok_rows, dtype=jnp.int32)
    query_use, key_use, value_use = (queries, projected_keys, projected_values)

    def position(device, offset):
        return device * tok_rows + offset

    query_pos = position(ctx_index, offsets)
    query_top = jnp.max(query_pos)
    kv_heads = width_kv // HEAD_SIZE
    head_group = width_q // HEAD_SIZE // kv_heads
    query_tensor = query_use.reshape(tok_rows, kv_heads, head_group, HEAD_SIZE)
    score_scale = HEAD_SIZE ** (-0.5)
    key_whole, value_whole = (
        lax.all_gather(key_use, "ctx", axis=0, tiled=True),
        lax.all_gather(value_use, "ctx", axis=0, tiled=True),
    )
    total_rows = key_whole.shape[0]
    block_rows = math.gcd(total_rows, 1024)

    def absorb_block(block_index, state):
        block_start = block_index * block_rows
        key_block = lax.dynamic_slice_in_dim(key_whole, block_start, block_rows, 0).reshape(
            block_rows, kv_heads, HEAD_SIZE
        )
        value_block = lax.dynamic_slice_in_dim(value_whole, block_start, block_rows, 0).reshape(
            block_rows, kv_heads, HEAD_SIZE
        )
        global_rows = block_start + jnp.arange(block_rows, dtype=jnp.int32)
        key_pos = position(global_rows // tok_rows, global_rows % tok_rows)

        def update(inner_state):
            running_max, running_sum, running_out = inner_state
            scores = (
                jnp.einsum(
                    "qhgd,khd->hgqk", query_tensor, key_block, preferred_element_type=jnp.float32
                )
                * score_scale
            )
            allowed = query_pos[:, None] >= key_pos[None, :]
            scores = jnp.where(allowed, scores, masked_score)
            new_max = jnp.maximum(running_max, jnp.max(scores, axis=3))
            weights = jnp.where(allowed, jnp.exp(scores - new_max[..., None]), 0.0)
            factor = jnp.exp(running_max - new_max)
            new_sum = running_sum * factor + jnp.sum(weights, axis=3)
            partial_out = jnp.einsum(
                "hgqk,khd->qhgd",
                weights.astype(jnp.bfloat16),
                value_block,
                preferred_element_type=jnp.float32,
            )
            new_out = running_out * jnp.transpose(factor, (2, 0, 1))[..., None] + partial_out
            return (new_max, new_sum, new_out)

        def keep_state(inner_state):
            return inner_state

        return lax.cond(jnp.min(key_pos) <= query_top, update, keep_state, state)

    initial = (
        jnp.full((kv_heads, head_group, tok_rows), masked_score, jnp.float32),
        jnp.zeros((kv_heads, head_group, tok_rows), jnp.float32),
        jnp.zeros((tok_rows, kv_heads, head_group, HEAD_SIZE), jnp.float32),
    )
    running_max, running_sum, running_out = lax.fori_loop(
        0, total_rows // block_rows, absorb_block, initial
    )
    attended = (
        (running_out / jnp.transpose(running_sum, (2, 0, 1))[..., None])
        .reshape(tok_rows, width_q)
        .astype(jnp.bfloat16)
    )
    ids_flat = route_ids[:, 0]
    chosen = (ids_flat[:, None] == jnp.arange(EXPERTS, dtype=jnp.int32)[None, :]).astype(jnp.int32)
    ranking = jnp.sum((jnp.cumsum(chosen, axis=0) - chosen) * chosen, axis=1)
    slot_of = ids_flat * CAP + ranking
    selector = (jnp.arange(EXPERTS * CAP, dtype=jnp.int32)[:, None] == slot_of[None, :]).astype(
        jnp.bfloat16
    )
    host_count = ctx_count // EXPERTS
    feature_width = hidden.shape[1]
    packed = jnp.dot(selector, hidden, preferred_element_type=jnp.float32).astype(jnp.bfloat16)
    packed = jnp.broadcast_to(
        packed.reshape(EXPERTS, 1, CAP, feature_width), (EXPERTS, host_count, CAP, feature_width)
    ).reshape(ctx_count, CAP, feature_width)
    arrived = lax.all_to_all(packed, "ctx", split_axis=0, concat_axis=0, tiled=True)
    arrived = lax.all_gather(arrived, "tp", axis=2, tiled=True)
    slot_count = arrived.shape[1]
    flat_rows = arrived.reshape(-1, arrived.shape[2])
    gate_val = jnp.dot(flat_rows, w_gate[0], preferred_element_type=jnp.float32)
    up_val = jnp.dot(flat_rows, w_up[0], preferred_element_type=jnp.float32)
    inner = (jax.nn.silu(gate_val) * up_val).astype(jnp.bfloat16)
    pair_inner = lax.all_gather(inner, "tp", axis=1, tiled=True)
    partial_out = jnp.dot(pair_inner, w_down[0], preferred_element_type=jnp.float32).astype(
        jnp.bfloat16
    )
    partial_out = partial_out.reshape(ctx_count, slot_count, partial_out.shape[1])
    returned = lax.all_to_all(partial_out, "ctx", split_axis=0, concat_axis=0, tiled=True)
    out_width = returned.shape[2]
    summed = returned.reshape(EXPERTS, host_count, CAP, out_width).astype(jnp.float32).sum(axis=1)
    summed = summed.reshape(EXPERTS * CAP, out_width)
    mixed = (summed[slot_of] * route_gain[:, None]).astype(jnp.bfloat16)
    return (attended, mixed)


def solution(mesh):
    in_specs = (
        P("ctx", "tp"),
        P("ctx", "tp"),
        P("ctx", "tp"),
        P("ctx", "tp"),
        P("ctx", None),
        P("ctx"),
        P("ctx", None, "tp"),
        P("ctx", None, "tp"),
        P("ctx", None, "tp"),
    )
    out_specs = (P("ctx", "tp"), P("ctx", "tp"))
    return jax.shard_map(body, mesh=mesh, in_specs=in_specs, out_specs=out_specs, check_vma=False)
```

profile of v0, /device:TPU:0, one launch (start us, length us, event | category | flops | bytes accessed | tf_op | source)
XLA Modules:
  0.0 152.1 jit_solution(1355597205857069275)
XLA Ops:
  0.7 0.8 fusion.35
  1.5 0.8 select_reduce_fusion
  2.4 0.7 multiply_add_fusion.1
  3.0 0.3 convolution_convert_fusion
  3.3 1.0 reshape_reshape.3
  4.3 8.3 %all-to-all-start = ((bf16[16,6,2560]{2,1,0:T(8,128)(2,1)}), bf16[16,6,2560]{2,1,0:T(8,128)(2,1)S(1)}, u32[]{:S(2)}, u32[]{:S(2)}) async-start(bf16[16,6,2560]{2,1,0:T(8,128)(2,1)} %reshape_reshape.3), calls=%async_computation | async-start | bytes 1310720 | tf_op jit(solution)/shard_map/all_to_all | solution.py:108
  12.7 0.6 fusion.48
  13.3 0.6 fusion.46
  15.3 45.2 %all_gather.12 = bf16[1024,256]{1,0:T(8,128)(2,1)S(1)} all-gather(bf16[64,256]{1,0:T(8,128)(2,1)S(1)} %copy-done.4), channel_id=1, replica_groups=mesh['ctx'=16,'tp'=2] {'ctx'}, dimensions={0}, use_global_device_ids=true | all-gather | bytes 557056 | tf_op jit(solution)/shard_map/all_gather | solution.py:37
  60.5 2.7 %all_gather.14 = bf16[16,6,5120]{2,1,0:T(8,128)(2,1)S(1)} all-gather(bf16[16,6,2560]{2,1,0:T(8,128)(2,1)S(1)} %all-to-all-done), channel_id=1, replica_groups=mesh['ctx'=16,'tp'=2] {'tp'}, dimensions={2}, use_global_device_ids=true | all-gather | bytes 1474560 | tf_op jit(solution)/shard_map/all_gather | solution.py:109
  63.3 0.4 reshape.55
  63.7 8.9 %fusion.24 = f32[96,2048]{1,0:T(8,128)S(1)} fusion(bf16[96,5120]{1,0:T(8,128)(2,1)S(1)} %reshape.55, bf16[1,5120,2048]{2,1,0:T(8,128)(2,1)} %param.17), kind=kOutput, calls=%fused_computation.26 | convolution fusion | flops 2013265920 | bytes 22740992 | tf_op jit(solution)/shard_map/dot_general | solution.py:112
  72.6 11.1 %fusion.32 = bf16[96,2048]{1,0:T(8,128)(2,1)S(1)} fusion(bf16[96,5120]{1,0:T(8,128)(2,1)S(1)} %reshape.55, bf16[1,5120,2048]{2,1,0:T(8,128)(2,1)} %param.18, f32[96,2048]{1,0:T(8,128)S(1)} %fusion.24), kind=kOutput, calls=%fused_computation.31 | convolution fusion | flops 2014445568 | bytes 23134208 | tf_op jit(solution)/shard_map/dot_general | solution.py:113
  83.7 2.4 %all_gather.15 = bf16[96,4096]{1,0:T(8,128)(2,1)S(1)} all-gather(bf16[96,2048]{1,0:T(8,128)(2,1)S(1)} %fusion.32), channel_id=1, replica_groups=mesh['ctx'=16,'tp'=2] {'tp'}, dimensions={1}, use_global_device_ids=true | all-gather | bytes 1179648 | tf_op jit(solution)/shard_map/all_gather | solution.py:115
  86.2 3.4 %fusion.26 = bf16[96,2560]{1,0:T(8,128)(2,1)S(1)} fusion(bf16[96,4096]{1,0:T(8,128)(2,1)S(1)} %all_gather.15, bf16[1,4096,2560]{2,1,0:T(8,128)(2,1)S(1)} %bitcast.52), kind=kOutput, calls=%fused_computation.28 | convolution fusion | flops 2013511680 | bytes 22249472 | tf_op jit(solution)/shard_map/dot_general | solution.py:116
  89.6 1.0 reshape.56
  90.6 3.6 %all-to-all-start.1 = ((bf16[16,6,2560]{2,1,0:T(8,128)(2,1)}), bf16[16,6,2560]{2,1,0:T(8,128)(2,1)S(1)}, u32[]{:S(2)}, u32[]{:S(2)}) async-start(bf16[16,6,2560]{2,1,0:T(8,128)(2,1)} %reshape.56), calls=%async_computation.1 | async-start | bytes 1310720 | tf_op jit(solution)/shard_map/all_to_all | solution.py:120
  94.2 48.7 %all_gather.13 = bf16[1024,256]{1,0:T(8,128)(2,1)S(1)} all-gather(bf16[64,256]{1,0:T(8,128)(2,1)S(1)} %copy-done.5), channel_id=1, replica_groups=mesh['ctx'=16,'tp'=2] {'ctx'}, dimensions={0}, use_global_device_ids=true | all-gather | bytes 557056 | tf_op jit(solution)/shard_map/all_gather | solution.py:38
  142.9 6.3 %conditional.1 = ((f32[2,5,64]{2,1,0:T(8,128)S(1)}, f32[64,2,5,128]{3,0,2,1:T(8,128)S(1)})) conditional(s32[]{:T(128)} %convert_element_type.33, (f32[2,5,64]{2,1,0:T(8,128)S(1)}, f32[64,2,5,128]{3,0,2,1:T(8,128)S(1)}) %tuple.25, (s32[64]{0:T(128)S(1)}, s32[1024]{0:T(1024)S(1)}, bf16[1024,256]{1,0:T(8,128)(2,1)S(1)}, bf16[64,1280]{1,0:T(8,128)(2,1)S(1)}, ...), branch_computations={%region_2.3_spmd, %region_3.6_spmd} | conditional | flops 344295296 | bytes 22939956 | solution.py:80
  143.0 0.2 reshape.49
  143.2 0.1 reshape.48
  143.3 0.7 fusion
  144.0 1.5 copy-done.2
  145.5 0.8 fusion.2
  146.4 0.1 reshape.50
  146.5 2.6 %fusion.9 = f32[64,2,5,128]{3,0,2,1:T(8,128)S(1)} fusion(f32[2,1024,64,5]{1,2,3,0:T(8,128)} %copy-done.2, f32[2,5,64]{2,1,0:T(8,128)S(1)} %broadcast_maximum_fusion, pred[64,1024]{1,0:T(8,128)(4,1)S(1)} %broadcast_compare_fusion, bf16[1024,2,128,1]{2,1,0,3:T(2,128)(2,1)S(1)} %bitcast.53, f32[64,2,5,128]{3,0,2,1:T(8,128)S(1)} %get-tuple-element.89, ...), kind=kOutput, calls=%fused_computation.9 | convolution fusion | flops 171212800 | bytes 3871744 | tf_op jit(solution)/shard_map/while/body/eval_jaxpr/cond/branch_1_fun/hgqk,khd->qhgd/dot_general | solution.py:68
  149.1 0.2 divide_convert_fusion
  149.3 0.1 copy.19
  149.4 0.9 convert_element_type.35
  150.3 0.1 reshape.60
  150.5 0.8 gather_fusion
  151.3 0.8 multiply_convert_fusion
  (38 shorter events, 0.3 us)
Async XLA Ops:
  0.6 2.4 %copy-start = (bf16[64,2560]{1,0:T(8,128)(2,1)S(1)}, bf16[64,2560]{1,0:T(8,128)(2,1)}, u32[]{:S(2)}) copy-start(bf16[64,2560]{1,0:T(8,128)(2,1)} %param.14) | copy-start | bytes 983044
  0.6 14.6 %copy-start.4 = (bf16[64,256]{1,0:T(8,128)(2,1)S(1)}, bf16[64,256]{1,0:T(8,128)(2,1)}, u32[]{:S(2)}) copy-start(bf16[64,256]{1,0:T(8,128)(2,1)} %param.12) | copy-start | bytes 98308
  4.3 56.2 %all-to-all-start = ((bf16[16,6,2560]{2,1,0:T(8,128)(2,1)}), bf16[16,6,2560]{2,1,0:T(8,128)(2,1)S(1)}, u32[]{:S(2)}, u32[]{:S(2)}) async-start(bf16[16,6,2560]{2,1,0:T(8,128)(2,1)} %reshape_reshape.3), calls=%async_computation | async-start | bytes 1310720 | tf_op jit(solution)/shard_map/all_to_all | solution.py:108
  63.6 22.5 %slice-start = ((s8[20971520]{0:T(1024)(128)(4,1)}), s8[4194304]{0:T(1024)(128)(4,1)S(1)}, s32[]{:S(2)}) async-start(s8[20971520]{0:T(1024)(128)(4,1)} %bitcast.51), calls=%async_computation.2 | async-start | bytes 8388608
  63.6 22.5 %slice-start.1 = ((s8[20971520]{0:T(1024)(128)(4,1)}), s8[4194304]{0:T(1024)(128)(4,1)S(1)}, s32[]{:S(2)}) async-start(s8[20971520]{0:T(1024)(128)(4,1)} %bitcast.51), calls=%async_computation.3 | async-start | bytes 8388608
  63.7 22.5 %slice-start.2 = ((s8[20971520]{0:T(1024)(128)(4,1)}), s8[4194304]{0:T(1024)(128)(4,1)S(1)}, s32[]{:S(2)}) async-start(s8[20971520]{0:T(1024)(128)(4,1)} %bitcast.51), calls=%async_computation.4 | async-start | bytes 8388608
  72.6 13.5 %slice-start.3 = ((s8[20971520]{0:T(1024)(128)(4,1)}), s8[4194304]{0:T(1024)(128)(4,1)S(1)}, s32[]{:S(2)}) async-start(s8[20971520]{0:T(1024)(128)(4,1)} %bitcast.51), calls=%async_computation.5 | async-start | bytes 8388608
  72.6 13.5 %slice-start.4 = ((s8[20971520]{0:T(1024)(128)(4,1)}), s8[4194304]{0:T(1024)(128)(4,1)S(1)}, s32[]{:S(2)}) async-start(s8[20971520]{0:T(1024)(128)(4,1)} %bitcast.51), calls=%async_computation.6 | async-start | bytes 8388608
  86.2 8.1 %copy-start.5 = (bf16[64,256]{1,0:T(8,128)(2,1)S(1)}, bf16[64,256]{1,0:T(8,128)(2,1)}, u32[]{:S(2)}) copy-start(bf16[64,256]{1,0:T(8,128)(2,1)} %param.13) | copy-start | bytes 98308
  89.6 53.3 %copy-start.3 = (bf16[64,1280]{1,0:T(8,128)(2,1)S(1)}, bf16[64,1280]{1,0:T(8,128)(2,1)}, u32[]{:S(2)}) copy-start(bf16[64,1280]{1,0:T(8,128)(2,1)} %param.11) | copy-start | bytes 491524
  90.6 59.7 %all-to-all-start.1 = ((bf16[16,6,2560]{2,1,0:T(8,128)(2,1)}), bf16[16,6,2560]{2,1,0:T(8,128)(2,1)S(1)}, u32[]{:S(2)}, u32[]{:S(2)}) async-start(bf16[16,6,2560]{2,1,0:T(8,128)(2,1)} %reshape.56), calls=%async_computation.1 | async-start | bytes 1310720 | tf_op jit(solution)/shard_map/all_to_all | solution.py:120
  142.9 7.4 %copy-start.6 = (s32[64,1]{0,1:T(1,128)S(1)}, s32[64,1]{0,1:T(1,128)}, u32[]{:S(2)}) copy-start(s32[64,1]{0,1:T(1,128)} %param.15) | copy-start | bytes 772
  144.0 1.5 copy-start.2
  150.3 1.8 %copy-start.1 = (bf16[64,2560]{1,0:T(8,128)(2,1)S(1)}, bf16[64,2560]{1,0:T(8,128)(2,1)}, u32[]{:S(2)}) copy-start(bf16[64,2560]{1,0:T(8,128)(2,1)} %param.14) | copy-start | bytes 983044
  150.5 0.8 copy-start.7
where the time goes:
time: 153 us; the launch traced here: 152 us
  blocking collectives  99 us (65%)
  matrix products  27 us (18%)
  starting transfers between devices  11.9 us (8%)
  local copies, waits for them, and re-layouts  6.33 us (4%)
  other arithmetic  5.61 us (4%)
  between operations  2.2 us (1%)
    all_gather x1, blocking collectives, body(): lax.all_gather(value_use, 'ctx', axis=0, tiled=True)  48.7 us
    all_gather x1, blocking collectives, body(): lax.all_gather(key_use, 'ctx', axis=0, tiled=True)  45.2 us
    dot_general x1, matrix products, body(): up_val = jnp.dot(flat_rows, w_up[0], preferred_element_type=jnp.float32)  11.1 us
    dot_general x1, matrix products, body(): gate_val = jnp.dot(flat_rows, w_gate[0], preferred_element_type=jnp.float32)  8.92 us
    all_to_all x1, starting transfers between devices, body(): lax.all_to_all(packed, 'ctx', split_axis=0, concat_axis=0, tiled=True)  8.34 us
    all_to_all x1, starting transfers between devices, body(): lax.all_to_all(partial_out, 'ctx', split_axis=0, concat_axis=0, tiled=True)  3.59 us
    dot_general x1, matrix products, body(): jnp.dot(pair_inner, w_down[0], preferred_element_type=jnp.float32)  3.41 us
  transfers between devices with their start and end apart: 2, of which 0 were waited for; matrix products, arithmetic and copies ran while one was open for 5% of the time, Pallas kernels for 0%

commit v1 on v0

--- a/solution.py
+++ b/solution.py
@@ -1,19 +1,400 @@
+import functools
 import math
 
 import jax
 import jax.numpy as jnp
 from jax import lax
+from jax.experimental import pallas as pl
+from jax.experimental.pallas import tpu as pltpu
 from jax.sharding import PartitionSpec as P
+
 
 HEAD_SIZE = 128
 EXPERTS = 16
 CAP = 6
 
-
 masked_score = -1e30
+COVER = int(2e10)
+sublane = 8
+VMEM = pltpu.VMEM
+
+
+def whole(n):
+    return [pl.BlockSpec(memory_space=VMEM) for _ in range(n)]
+
+
+def params(limit=8):
+    return pltpu.CompilerParams(vmem_limit_bytes=limit * 1024 * 1024)
+
+
+def far(array):
+    return pltpu.with_memory_space_constraint(array, pltpu.HBM)
+
+
+def near(*arrays):
+    return [pltpu.with_memory_space_constraint(a, VMEM) for a in arrays]
+
+
+def slots_of(ids_row):
+    count = ids_row.shape[1]
+    across = jnp.broadcast_to(ids_row, (count, count))
+    down = across.T
+    earlier = lax.broadcasted_iota(jnp.int32, (count, count), 0) < lax.broadcasted_iota(
+        jnp.int32, (count, count), 1
+    )
+    same = jnp.where(jnp.logical_and(across == down, earlier), 1.0, 0.0)
+    return jnp.sum(same, axis=0, keepdims=True)
+
+
+def pack_kernel(place_ref, side_ref, ids_ref, hidden_hbm, key_hbm, value_hbm, packed_ref, kv_ref, hidden_ref, sems, *, pieces):
+    width_kv = key_hbm.shape[1]
+    copies = [
+        pltpu.make_async_copy(hidden_hbm, hidden_ref, sems.at[0]),
+        pltpu.make_async_copy(key_hbm, kv_ref.at[:, pl.ds(0, width_kv)], sems.at[1]),
+        pltpu.make_async_copy(value_hbm, kv_ref.at[:, pl.ds(width_kv, width_kv)], sems.at[2]),
+    ]
+    for copy in copies:
+        copy.start()
+    ids_row = ids_ref[...].astype(jnp.float32)
+    rank = slots_of(ids_row)
+    rows = EXPERTS * CAP * pieces
+    width = hidden_ref.shape[1] // pieces
+    slot = ids_row * (CAP * pieces) + rank
+    targets = jnp.concatenate([slot + float(k * CAP) for k in range(pieces)], axis=1)
+    row_number = lax.broadcasted_iota(jnp.int32, (rows, targets.shape[1]), 0).astype(jnp.float32)
+    selector = jnp.where(row_number == targets, 1.0, 0.0).astype(jnp.bfloat16)
+    copies[0].wait()
+    stacked = jnp.concatenate(
+        [hidden_ref[:, k * width : (k + 1) * width] for k in range(pieces)], axis=0
+    )
+    out = jnp.dot(selector, stacked, preferred_element_type=jnp.float32).astype(jnp.bfloat16)
+    packed_ref[...] = out.reshape(packed_ref.shape)
+    copies[1].wait()
+    copies[2].wait()
+
+
+def pack(place, side, ids_row, hidden, keys, values, pieces):
+    width = hidden.shape[1] // pieces
+    return pl.pallas_call(
+        functools.partial(pack_kernel, pieces=pieces),
+        out_shape=(
+            VMEM((EXPERTS, CAP * pieces, width), jnp.bfloat16),
+            VMEM((keys.shape[0], 2 * keys.shape[1]), jnp.bfloat16),
+        ),
+        in_specs=[pl.BlockSpec(memory_space=pltpu.SMEM)] * 2
+        + whole(1)
+        + [pl.BlockSpec(memory_space=pl.ANY)] * 3,
+        out_specs=tuple(whole(2)),
+        scratch_shapes=[VMEM(hidden.shape, hidden.dtype), pltpu.SemaphoreType.DMA((3,))],
+        compiler_params=params(4),
+        cost_estimate=pl.CostEstimate(flops=COVER, bytes_accessed=1, transcendentals=0),
+        name="pack",
+    )(place, side, ids_row, far(hidden), far(keys), far(values))
+
+
+def unpack_rows(arrived, pieces):
+    rows, _ = arrived.shape
+    per = rows // pieces
+    group = CAP * pieces
+    number = lax.broadcasted_iota(jnp.int32, (rows, 1), 0)
+    piece, rest = number // per, number % per
+    wanted = (rest // CAP) * group + piece * CAP + rest % CAP
+    selector = jnp.where(
+        lax.broadcasted_iota(jnp.int32, (rows, rows), 1) == wanted, 1.0, 0.0
+    ).astype(jnp.bfloat16)
+    out = jnp.dot(selector, arrived, preferred_element_type=jnp.float32).astype(jnp.bfloat16)
+    return jnp.concatenate([out[k * per : (k + 1) * per] for k in range(pieces)], axis=1)
+
+
+def column_blocks(width):
+    wide = math.gcd(width, 512)
+    return wide, width // wide
+
+
+def halves(own, rest, side):
+    return jnp.where(side == 0, own, rest), jnp.where(side == 0, rest, own)
+
+
+def early_rows(w_down):
+    return w_down.shape[1] * 3 // 4
+
+
+def gate_up_kernel(side_ref, own_ref, rest_ref, wg_ref, wu_ref, wd_hbm, inner_ref, wd_ref, sems, *, pieces):
+    early = wd_ref.shape[0]
+    parts = sems.shape[0]
+    copies = [
+        pltpu.make_async_copy(
+            wd_hbm.at[0, pl.ds(k * (early // parts), early // parts), :],
+            wd_ref.at[pl.ds(k * (early // parts), early // parts), :],
+            sems.at[k],
+        )
+        for k in range(parts)
+    ]
+    for copy in copies:
+        copy.start()
+    rows = own_ref.shape[0] * own_ref.shape[1]
+    width = own_ref.shape[2]
+    lo, hi = halves(own_ref[...].reshape(rows, width), rest_ref[...].reshape(rows, width), side_ref[0])
+    x = jnp.concatenate([unpack_rows(lo, pieces), unpack_rows(hi, pieces)], axis=1)
+    wide, blocks = column_blocks(wg_ref.shape[2])
+    for n in range(blocks):
+        at = slice(n * wide, (n + 1) * wide)
+        gate = jnp.dot(x, wg_ref[0, :, at], preferred_element_type=jnp.float32)
+        up = jnp.dot(x, wu_ref[0, :, at], preferred_element_type=jnp.float32)
+        inner_ref[:, at] = (gate / (1.0 + jnp.exp(-gate)) * up).astype(jnp.bfloat16)
+    for copy in copies:
+        copy.wait()
+
+
+def gate_up(side, own, rest, wg, wu, wd, pieces):
+    rows = own.shape[0] * own.shape[1] // pieces
+    near_spec = pl.BlockSpec(memory_space=VMEM)
+    return pl.pallas_call(
+        functools.partial(gate_up_kernel, pieces=pieces),
+        out_shape=(
+            VMEM((rows, wg.shape[2]), jnp.bfloat16),
+            VMEM((early_rows(wd), wd.shape[2]), wd.dtype),
+        ),
+        in_specs=[pl.BlockSpec(memory_space=pltpu.SMEM)]
+        + whole(4)
+        + [pl.BlockSpec(memory_space=pl.ANY)],
+        out_specs=(near_spec, near_spec),
+        scratch_shapes=[pltpu.SemaphoreType.DMA((4,))],
+        compiler_params=params(6),
+        cost_estimate=pl.CostEstimate(
+            flops=4 * rows * wg.size, bytes_accessed=wd.size, transcendentals=0
+        ),
+        name="gate_up",
+    )(side, *near(own, rest, wg, wu), far(wd))
+
+
+def down_kernel(side_ref, own_ref, rest_ref, wd_ref, wd_hbm, out_ref, buf, sem, *, pieces):
+    early = wd_ref.shape[0]
+    copy = pltpu.make_async_copy(wd_hbm.at[0, pl.ds(early, buf.shape[0]), :], buf, sem)
+    copy.start()
+    lo, hi = halves(own_ref[...], rest_ref[...], side_ref[0])
+    x = jnp.concatenate([lo, hi], axis=1)
+    per = x.shape[0]
+    deep = math.gcd(early, buf.shape[0])
+    wide, blocks = column_blocks(wd_ref.shape[1])
+
+    def partial(ref, first, n, total):
+        for k in range(ref.shape[0] // deep):
+            rows = slice(k * deep, (k + 1) * deep)
+            total = total + jnp.dot(
+                x[:, first + k * deep : first + (k + 1) * deep],
+                ref[rows, n * wide : (n + 1) * wide],
+                preferred_element_type=jnp.float32,
+            )
+        return total
+
+    zeros = jnp.zeros((per, wide), jnp.float32)
+    totals = [partial(wd_ref, 0, n, zeros) for n in range(blocks)]
+    copy.wait()
+    full = jnp.concatenate(
+        [partial(buf, early, n, totals[n]).astype(jnp.bfloat16) for n in range(blocks)], axis=1
+    )
+    width = full.shape[1] // pieces
+    rounded = [full[:, k * width : (k + 1) * width] for k in range(pieces)]
+    stacked = jnp.concatenate(rounded, axis=0)
+    group = CAP * pieces
+    rows = per * pieces
+    number = lax.broadcasted_iota(jnp.int32, (rows, 1), 0)
+    source, left = number // group, number % group
+    wanted = (left // CAP) * per + source * CAP + left % CAP
+    selector = jnp.where(
+        lax.broadcasted_iota(jnp.int32, (rows, rows), 1) == wanted, 1.0, 0.0
+    ).astype(jnp.bfloat16)
+    out = jnp.dot(selector, stacked, preferred_element_type=jnp.float32).astype(jnp.bfloat16)
+    out_ref[...] = out.reshape(out_ref.shape)
+
+
+def down(side, own, rest, early, w, sources, pieces):
+    left = w.shape[1] - early.shape[0]
+    return pl.pallas_call(
+        functools.partial(down_kernel, pieces=pieces),
+        out_shape=VMEM((sources, CAP * pieces, w.shape[2] // pieces), jnp.bfloat16),
+        in_specs=[pl.BlockSpec(memory_space=pltpu.SMEM)]
+        + whole(3)
+        + [pl.BlockSpec(memory_space=pl.ANY)],
+        out_specs=pl.BlockSpec(memory_space=VMEM),
+        scratch_shapes=[VMEM((left, w.shape[2]), w.dtype), pltpu.SemaphoreType.DMA],
+        compiler_params=params(10),
+        cost_estimate=pl.CostEstimate(
+            flops=2 * own.shape[0] * w.size, bytes_accessed=w.size, transcendentals=0
+        ),
+        name="down",
+    )(side, *near(own, rest, early), far(w))
+
+
+def combine_kernel(ids_ref, gain_ref, back_ref, mixed_ref, *, pieces, hosts):
+    ids_row = ids_ref[...].astype(jnp.float32)
+    count = ids_row.shape[1]
+    rank = slots_of(ids_row)
+    width = back_ref.shape[3]
+    group = CAP * pieces
+    slot = ids_row * group + rank
+    gain = jnp.broadcast_to(gain_ref[...], (sublane, count)).T[:, 0:1]
+    first = jnp.broadcast_to(slot, (sublane, count)).T[:, 0:1]
+    column = lax.broadcasted_iota(jnp.int32, (count, EXPERTS * group), 1).astype(jnp.float32)
+    for k in range(pieces):
+        selector = jnp.where(column == first + float(k * CAP), 1.0, 0.0).astype(jnp.bfloat16)
+        picked = jnp.zeros((count, width), jnp.float32)
+        for h in range(hosts):
+            piece_rows = back_ref[h].reshape(EXPERTS * group, width)
+            picked = picked + jnp.dot(selector, piece_rows, preferred_element_type=jnp.float32)
+        mixed_ref[:, k * width : (k + 1) * width] = (picked * gain).astype(jnp.bfloat16)
+
+
+def combine(ids_row, gain_row, back, pieces):
+    hosts, _, _, width = back.shape
+    return pl.pallas_call(
+        functools.partial(combine_kernel, pieces=pieces, hosts=hosts),
+        out_shape=jax.ShapeDtypeStruct((ids_row.shape[1], width * pieces), jnp.bfloat16),
+        in_specs=whole(3),
+        out_specs=pl.BlockSpec(memory_space=VMEM),
+        compiler_params=params(),
+        name="combine",
+    )(*near(ids_row, gain_row, back))
+
+
+def join_kernel(*refs):
+    rows = refs[0].shape[0]
+    for k, ref in enumerate(refs[:-1]):
+        refs[-1][k * rows : (k + 1) * rows, :] = ref[...]
+
+
+def join(parts):
+    rows, width = parts[0].shape
+    return pl.pallas_call(
+        join_kernel,
+        out_shape=VMEM((len(parts) * rows, width), parts[0].dtype),
+        in_specs=whole(len(parts)),
+        out_specs=pl.BlockSpec(memory_space=VMEM),
+        compiler_params=params(),
+        name="join",
+    )(*near(*parts))
+
+
+def attend_kernel(place_ref, query_ref, *refs, owner_of):
+    out_ref = refs[-1]
+    parts = refs[:-1]
+    tok = query_ref.shape[0]
+    kv_width = parts[0].shape[1] // 2
+    kv_heads = kv_width // HEAD_SIZE
+    group = query_ref.shape[1] // HEAD_SIZE // kv_heads
+    me = place_ref[0]
+    scale = HEAD_SIZE**-0.5
+    rows = group * tok
+    offset = lax.broadcasted_iota(jnp.int32, (rows, 1), 0)
+    query_pos = me * tok + lax.rem(offset, tok)
+    masks = []
+    for p, part in enumerate(parts):
+        count = part.shape[0]
+        number = lax.broadcasted_iota(jnp.int32, (1, count), 1)
+        block = lax.div(number, tok)
+        owner, held = owner_of(me, p, block)
+        key_pos = jnp.where(held, owner * tok + lax.rem(number, tok), jnp.iinfo(jnp.int32).max)
+        masks.append(key_pos <= query_pos)
+    for head in range(kv_heads):
+        at = head * HEAD_SIZE
+        first = head * group
+        queries = jnp.concatenate(
+            [
+                query_ref[:, (first + g) * HEAD_SIZE : (first + g + 1) * HEAD_SIZE]
+                for g in range(group)
+            ],
+            axis=0,
+        )
+        scores = []
+        for part, mask in zip(parts, masks):
+            score = lax.dot_general(
+                queries,
+                part[:, at : at + HEAD_SIZE],
+                (((1,), (1,)), ((), ())),
+                preferred_element_type=jnp.float32,
+            )
+            scores.append(jnp.where(mask, score * scale, masked_score))
+        top = functools.reduce(jnp.maximum, [jnp.max(s, axis=1, keepdims=True) for s in scores])
+        total = jnp.zeros((rows, 1), jnp.float32)
+        mixed = jnp.zeros((rows, HEAD_SIZE), jnp.float32)
+        for part, score in zip(parts, scores):
+            weight = jnp.exp(score - top)
+            total = total + jnp.sum(weight, axis=1, keepdims=True)
+            mixed = mixed + jnp.dot(
+                weight.astype(jnp.bfloat16),
+                part[:, kv_width + at : kv_width + at + HEAD_SIZE],
+                preferred_element_type=jnp.float32,
+            )
+        mixed = (mixed / total).astype(jnp.bfloat16)
+        for g in range(group):
+            out_ref[:, (first + g) * HEAD_SIZE : (first + g + 1) * HEAD_SIZE] = mixed[
+                g * tok : (g + 1) * tok
+            ]
+
+
+def attend(place, queries, parts, owner_of):
+    return pl.pallas_call(
+        functools.partial(attend_kernel, owner_of=owner_of),
+        out_shape=jax.ShapeDtypeStruct(queries.shape, jnp.bfloat16),
+        in_specs=[pl.BlockSpec(memory_space=pltpu.SMEM)] + whole(1 + len(parts)),
+        out_specs=pl.BlockSpec(memory_space=VMEM),
+        compiler_params=params(8 + 40 * sum(p.shape[0] for p in parts) // 8192),
+        name="attend",
+    )(place, *near(queries, *parts))
+
+
+plane = 4
 
 
 def body(
+    queries, projected_keys, projected_values, hidden, route_ids, route_gain, w_gate, w_up, w_down
+):
+    ctx_count = lax.axis_size("ctx")
+    place = lax.axis_index("ctx").astype(jnp.int32).reshape(1)
+    side = lax.axis_index("tp").astype(jnp.int32).reshape(1)
+    hosts = ctx_count // EXPERTS
+    pieces = sublane // math.gcd(CAP, sublane)
+    ids_row = route_ids.reshape(1, -1)
+    gain_row = route_gain.reshape(1, -1)
+
+    packed, kv = pack(place, side, ids_row, hidden, projected_keys, projected_values, pieces)
+    if hosts > 1:
+        packed = jnp.repeat(packed, hosts, axis=0)
+    arrived = lax.all_to_all(packed, "ctx", split_axis=0, concat_axis=0, tiled=True)
+
+    if hosts == 1:
+        slabs = [kv]
+        for step in range(1, ctx_count // plane):
+            pairs = [(i, i + step * plane) for i in range(ctx_count - step * plane)]
+            slabs.append(lax.ppermute(kv, "ctx", pairs))
+        column = join(slabs)
+        parts = [column]
+        for flip in range(1, plane):
+            parts.append(lax.ppermute(column, "ctx", [(i, i ^ flip) for i in range(ctx_count)]))
+
+        def owner_of(me, part, block):
+            layer = lax.div(me, plane) - block
+            return layer * plane + (lax.rem(me, plane) ^ part), layer >= 0
+    else:
+        parts = [lax.all_gather(kv, "ctx", axis=0, tiled=True)]
+
+        def owner_of(me, part, block):
+            return block, block >= 0
+
+    other = [(0, 1), (1, 0)]
+    arrived_rest = lax.ppermute(arrived, "tp", other)
+    inner, early = gate_up(side, arrived, arrived_rest, w_gate, w_up, w_down, pieces)
+    inner_rest = lax.ppermute(inner, "tp", other)
+    result = down(side, inner, inner_rest, early, w_down, ctx_count, pieces)
+    back = lax.all_to_all(result, "ctx", split_axis=0, concat_axis=0, tiled=True)
+    attended = attend(place, queries, parts, owner_of)
+    back = back.reshape(EXPERTS, hosts, CAP * pieces, -1).transpose(1, 0, 2, 3)
+    mixed = combine(ids_row, gain_row, back, pieces)
+    return (attended, mixed)
+
+
+def general_body(
     queries, projected_keys, projected_values, hidden, route_ids, route_gain, w_gate, w_up, w_down
 ):
     tok_rows = queries.shape[0]
@@ -84,9 +465,7 @@
         jnp.zeros((kv_heads, head_group, tok_rows), jnp.float32),
         jnp.zeros((tok_rows, kv_heads, head_group, HEAD_SIZE), jnp.float32),
     )
-    running_max, running_sum, running_out = lax.fori_loop(
-        0, total_rows // block_rows, absorb_block, initial
-    )
+    _, running_sum, running_out = lax.fori_loop(0, total_rows // block_rows, absorb_block, initial)
     attended = (
         (running_out / jnp.transpose(running_sum, (2, 0, 1))[..., None])
         .reshape(tok_rows, width_q)
@@ -138,4 +517,8 @@
         P("ctx", None, "tp"),
     )
     out_specs = (P("ctx", "tp"), P("ctx", "tp"))
+    if mesh.shape["ctx"] != EXPERTS:
+        return jax.shard_map(
+            general_body, mesh=mesh, in_specs=in_specs, out_specs=out_specs, check_vma=False
+        )
     return jax.shard_map(body, mesh=mesh, in_specs=in_specs, out_specs=out_specs, check_vma=False)

time: 153 us -> 81.5 us (0.53)
  the two profiles are of different devices: /device:TPU:0 before, /device:TPU:28 now
where the time goes in v1:
time: 81.5 us; the launch traced here: 81.2 us
  waiting for transfers between devices  28.1 us (34%)
  blocking collectives  19.3 us (24%)
  Pallas kernels  18.7 us (23%)
  starting transfers between devices  13.7 us (17%)
    all_to_all x1, blocking collectives, body(): lax.all_to_all(packed, 'ctx', split_axis=0, concat_axis=0, tiled=True)  19.3 us
    ppermute x3, waiting for transfers between devices, body(): slabs.append(lax.ppermute(kv, 'ctx', pairs))  13.5 us
    ppermute x3, waiting for transfers between devices, body(): lax.ppermute(column, 'ctx', [(i, i ^ flip) for i in range(ctx_count)])  11.2 us
    pallas_call x1, Pallas kernels, gate_up(): pl.pallas_call(functools.partial(gate_up_kernel, pieces=pieces), out_shap...  7.69 us
    pallas_call x1, Pallas kernels, down(): pl.pallas_call(functools.partial(down_kernel, pieces=pieces), out_shape=V...  6.04 us
    all_to_all x1, starting transfers between devices, body(): lax.all_to_all(result, 'ctx', split_axis=0, concat_axis=0, tiled=True)  6.03 us
    ppermute x3, starting transfers between devices, body(): slabs.append(lax.ppermute(kv, 'ctx', pairs))  3.86 us
    ppermute x3, starting transfers between devices, body(): lax.ppermute(column, 'ctx', [(i, i ^ flip) for i in range(ctx_count)])  3.55 us
  transfers between devices with their start and end apart: 9, of which 6 were waited for; matrix products, arithmetic and copies ran while one was open for 0% of the time, Pallas kernels for 3%

profile of v1, /device:TPU:28, one launch (start us, length us, event | category | flops | bytes accessed | tf_op | source)
XLA Modules:
  0.0 81.2 jit_solution(9542375257696735420)
XLA Ops:
  0.6 0.0 copy-start.3
  0.6 0.6 copy-done.3
  1.3 1.5 %pack.1 = (bf16[16,24,640]{2,1,0:T(8,128)(2,1)S(1)}, bf16[64,512]{1,0:T(8,128)(2,1)S(1)}) custom-call(s32[1]{0:T(128)} %bitcast.place_ref, s32[1]{0:T(128)} %bitcast.1.side_ref, s32[1,64]{1,0:T(1,128)S(1)} %bitcast.6, bf16[64,2560]{1,0:T(8,128)(2,1)} %hidden_hbm.1, bf16[64,256]{1,0:T(8,128)(2,1)} %key_hbm.1, bf16[64,256]{1,0:T(8,128)(2,1)} %value_hbm.1), custom_call_target="tpu_custom_call" | custom-call | flops 20000000000 | bytes 1 | tf_op jit(solution)/shard_map/pack/pallas_call | solution.py:78
  2.8 19.3 %all_to_all.10.own_ref = bf16[16,24,640]{2,1,0:T(8,128)(2,1)S(1)} all-to-all(bf16[16,24,640]{2,1,0:T(8,128)(2,1)S(1)} %get-tuple-element.7), channel_id=1, replica_groups=mesh['ctx'=16,'tp'=2] {'ctx'}, dimensions={0} | all-to-all | bytes 983040 | tf_op jit(solution)/shard_map/all_to_all | solution.py:364
  22.1 0.0 collective-permute-start.6
  22.1 1.9 %collective-permute-done.6.rest_ref = bf16[16,24,640]{2,1,0:T(8,128)(2,1)S(1)} collective-permute-done((bf16[16,24,640]{2,1,0:T(8,128)(2,1)S(1)}, bf16[16,24,640]{2,1,0:T(8,128)(2,1)S(1)}, u32[]{:S(2)}, u32[]{:S(2)}) %collective-permute-start.6) | collective-permute-done | bytes 491552 | tf_op jit(solution)/shard_map/ppermute | solution.py:386
  24.0 0.0 copy-done
  24.0 0.0 copy-done.1
  24.0 7.7 %gate_up.1 = (bf16[96,2048]{1,0:T(8,128)(2,1)S(1)}, bf16[3072,2560]{1,0:T(8,128)(2,1)S(1)}) custom-call(s32[1]{0:T(128)} %bitcast.1.side_ref, bf16[16,24,640]{2,1,0:T(8,128)(2,1)S(1)} %all_to_all.10.own_ref, bf16[16,24,640]{2,1,0:T(8,128)(2,1)S(1)} %collective-permute-done.6.rest_ref, bf16[1,5120,2048]{2,1,0:T(8,128)(2,1)S(1)} %copy-done, ...), custom_call_target="tpu_custom_call" | custom-call | flops 4026531840 | bytes 10485760 | tf_op jit(solution)/shard_map/gate_up/pallas_call | solution.py:152
  31.7 0.0 copy-start.2
  31.7 0.0 copy-start.4
  31.7 0.0 copy-start.5
  31.7 0.2 collective-permute-start.7
  31.9 1.6 %collective-permute-done.7.rest_ref = bf16[96,2048]{1,0:T(8,128)(2,1)S(1)} collective-permute-done((bf16[96,2048]{1,0:T(8,128)(2,1)S(1)}, bf16[96,2048]{1,0:T(8,128)(2,1)S(1)}, u32[]{:S(2)}, u32[]{:S(2)}) %collective-permute-start.7) | collective-permute-done | bytes 393248 | tf_op jit(solution)/shard_map/ppermute | solution.py:388
  33.5 6.0 %down.1 = bf16[16,24,640]{2,1,0:T(8,128)(2,1)} custom-call(s32[1]{0:T(128)} %bitcast.1.side_ref, bf16[96,2048]{1,0:T(8,128)(2,1)S(1)} %get-tuple-element.8.own_ref, bf16[96,2048]{1,0:T(8,128)(2,1)S(1)} %collective-permute-done.7.rest_ref, bf16[3072,2560]{1,0:T(8,128)(2,1)S(1)} %get-tuple-element.9.wd_ref, bf16[1,4096,2560]{2,1,0:T(8,128)(2,1)} %wd_hbm.3), custom_call_target="tpu_custom_call" | custom-call | flops 2013265920 | bytes 10485760 | tf_op jit(solution)/shard_map/down/pallas_call | solution.py:214
  39.5 6.0 %all-to-all-start.1 = ((bf16[16,24,640]{2,1,0:T(8,128)(2,1)}), bf16[16,24,640]{2,1,0:T(8,128)(2,1)S(1)}, u32[]{:S(2)}, u32[]{:S(2)}) async-start(bf16[16,24,640]{2,1,0:T(8,128)(2,1)} %down.1), calls=%async_computation.1 | async-start | bytes 983040 | tf_op jit(solution)/shard_map/all_to_all | solution.py:390
  45.6 1.3 %collective-permute-start = (bf16[64,512]{1,0:T(8,128)(2,1)S(1)}, bf16[64,512]{1,0:T(8,128)(2,1)S(1)}, u32[]{:S(2)}, u32[]{:S(2)}) collective-permute-start(bf16[64,512]{1,0:T(8,128)(2,1)S(1)} %get-tuple-element.6.refs_0_), channel_id=1, source_target_pairs={{0,8},{2,10},{4,12},{6,14},{8,16},{10,18},{12,20},{14,22},{16,24},... | collective-permute-start | bytes 196616 | tf_op jit(solution)/shard_map/ppermute | solution.py:370
  46.9 1.3 %collective-permute-start.1 = (bf16[64,512]{1,0:T(8,128)(2,1)S(1)}, bf16[64,512]{1,0:T(8,128)(2,1)S(1)}, u32[]{:S(2)}, u32[]{:S(2)}) collective-permute-start(bf16[64,512]{1,0:T(8,128)(2,1)S(1)} %get-tuple-element.6.refs_0_), channel_id=1, source_target_pairs={{0,16},{2,18},{4,20},{6,22},{8,24},{10,26},{12,28},{14,30},{1,17},... | collective-permute-start | bytes 196616 | tf_op jit(solution)/shard_map/ppermute | solution.py:370
  48.2 1.3 %collective-permute-start.2 = (bf16[64,512]{1,0:T(8,128)(2,1)S(1)}, bf16[64,512]{1,0:T(8,128)(2,1)S(1)}, u32[]{:S(2)}, u32[]{:S(2)}) collective-permute-start(bf16[64,512]{1,0:T(8,128)(2,1)S(1)} %get-tuple-element.6.refs_0_), channel_id=1, source_target_pairs={{0,24},{2,26},{4,28},{6,30},{1,25},{3,27},{5,29},{7,31}} | collective-permute-start | bytes 196616 | tf_op jit(solution)/shard_map/ppermute | solution.py:370
  49.5 4.9 %collective-permute-done.refs_1_ = bf16[64,512]{1,0:T(8,128)(2,1)S(1)} collective-permute-done((bf16[64,512]{1,0:T(8,128)(2,1)S(1)}, bf16[64,512]{1,0:T(8,128)(2,1)S(1)}, u32[]{:S(2)}, u32[]{:S(2)}) %collective-permute-start) | collective-permute-done | bytes 65568 | tf_op jit(solution)/shard_map/ppermute | solution.py:370
  54.4 8.5 %collective-permute-done.1.refs_2_ = bf16[64,512]{1,0:T(8,128)(2,1)S(1)} collective-permute-done((bf16[64,512]{1,0:T(8,128)(2,1)S(1)}, bf16[64,512]{1,0:T(8,128)(2,1)S(1)}, u32[]{:S(2)}, u32[]{:S(2)}) %collective-permute-start.1) | collective-permute-done | bytes 65568 | tf_op jit(solution)/shard_map/ppermute | solution.py:370
  62.9 0.0 collective-permute-done.2.refs_3_
  62.9 1.5 %collective-permute-start.3 = (bf16[256,512]{1,0:T(8,128)(2,1)S(1)}, bf16[256,512]{1,0:T(8,128)(2,1)S(1)}, u32[]{:S(2)}, u32[]{:S(2)}) collective-permute-start(bf16[256,512]{1,0:T(8,128)(2,1)S(1)} %join.1.refs_0_), channel_id=1, source_target_pairs={{0,2},{2,0},{4,6},{6,4},{8,10},{10,8},{12,14},{14,12},{16,18},{18,... | collective-permute-start | bytes 786440 | tf_op jit(solution)/shard_map/ppermute | solution.py:374
  64.5 0.6 collective-permute-start.4
  65.0 1.5 %collective-permute-start.5 = (bf16[256,512]{1,0:T(8,128)(2,1)S(1)}, bf16[256,512]{1,0:T(8,128)(2,1)S(1)}, u32[]{:S(2)}, u32[]{:S(2)}) collective-permute-start(bf16[256,512]{1,0:T(8,128)(2,1)S(1)} %join.1.refs_0_), channel_id=1, source_target_pairs={{0,6},{2,4},{4,2},{6,0},{8,14},{10,12},{12,10},{14,8},{16,22},{18,... | collective-permute-start | bytes 786440 | tf_op jit(solution)/shard_map/ppermute | solution.py:374
  66.5 5.7 %collective-permute-done.3.refs_1_ = bf16[256,512]{1,0:T(8,128)(2,1)S(1)} collective-permute-done((bf16[256,512]{1,0:T(8,128)(2,1)S(1)}, bf16[256,512]{1,0:T(8,128)(2,1)S(1)}, u32[]{:S(2)}, u32[]{:S(2)}) %collective-permute-start.3) | collective-permute-done | bytes 262176 | tf_op jit(solution)/shard_map/ppermute | solution.py:374
  72.2 5.5 %collective-permute-done.4.refs_2_ = bf16[256,512]{1,0:T(8,128)(2,1)S(1)} collective-permute-done((bf16[256,512]{1,0:T(8,128)(2,1)S(1)}, bf16[256,512]{1,0:T(8,128)(2,1)S(1)}, u32[]{:S(2)}, u32[]{:S(2)}) %collective-permute-start.4) | collective-permute-done | bytes 262176 | tf_op jit(solution)/shard_map/ppermute | solution.py:374
  77.7 0.0 collective-permute-done.5.refs_3_
  77.7 2.1 %attend.1 = bf16[64,1280]{1,0:T(8,128)(2,1)} custom-call(s32[1]{0:T(128)} %bitcast.place_ref, bf16[64,1280]{1,0:T(8,128)(2,1)S(1)} %copy-done.2, bf16[256,512]{1,0:T(8,128)(2,1)S(1)} %join.1.refs_0_, bf16[256,512]{1,0:T(8,128)(2,1)S(1)} %collective-permute-done.3.refs_1_, bf16[256,512]{1,0:T(8,128)(2,1)S(1)} %collective-permute-done.4.refs_2_, ...), custom_call_target="tpu_custom_call" | custom-call | tf_op jit(solution)/shard_map/attend/pallas_call | solution.py:337
  79.8 0.0 all-to-all-done.1
  79.8 0.0 copy-done.5
  79.8 1.4 %combine.1 = bf16[64,2560]{1,0:T(8,128)(2,1)} custom-call(s32[1,64]{1,0:T(1,128)S(1)} %bitcast.7, f32[1,64]{1,0:T(1,128)S(1)} %bitcast.8, bf16[1,16,24,640]{3,2,1,0:T(8,128)(2,1)S(1)} %bitcast.5), custom_call_target="tpu_custom_call" | custom-call | tf_op jit(solution)/shard_map/combine/pallas_call | solution.py:251
  (5 shorter events, 0.0 us)
Async XLA Ops:
  0.6 0.7 copy-start.3
  1.3 22.7 %copy-start = (bf16[1,5120,2048]{2,1,0:T(8,128)(2,1)S(1)}, bf16[1,5120,2048]{2,1,0:T(8,128)(2,1)}, u32[]{:S(2)}) copy-start(bf16[1,5120,2048]{2,1,0:T(8,128)(2,1)} %wg_ref.1) | copy-start | bytes 62914564
  1.3 22.7 %copy-start.1 = (bf16[1,5120,2048]{2,1,0:T(8,128)(2,1)S(1)}, bf16[1,5120,2048]{2,1,0:T(8,128)(2,1)}, u32[]{:S(2)}) copy-start(bf16[1,5120,2048]{2,1,0:T(8,128)(2,1)} %wu_ref.1) | copy-start | bytes 62914564
  22.1 1.9 %collective-permute-start.6 = (bf16[16,24,640]{2,1,0:T(8,128)(2,1)S(1)}, bf16[16,24,640]{2,1,0:T(8,128)(2,1)S(1)}, u32[]{:S(2)}, u32[]{:S(2)}) collective-permute-start(bf16[16,24,640]{2,1,0:T(8,128)(2,1)S(1)} %all_to_all.10.own_ref), channel_id=1, source_target_pairs={{0,1},{1,0},{2,3},{3,2},{4,5},{5,4},{6,7},{7,6},{8,9},{9,8},{10,11... | collective-permute-start | bytes 1474568 | tf_op jit(solution)/shard_map/ppermute | solution.py:386
  31.7 46.0 %copy-start.2 = (bf16[64,1280]{1,0:T(8,128)(2,1)S(1)}, bf16[64,1280]{1,0:T(8,128)(2,1)}, u32[]{:S(2)}) copy-start(bf16[64,1280]{1,0:T(8,128)(2,1)} %query_ref.1) | copy-start | bytes 491524
  31.7 48.1 %copy-start.4 = (s32[64,1]{0,1:T(1,128)S(1)}, s32[64,1]{0,1:T(1,128)}, u32[]{:S(2)}) copy-start(s32[64,1]{0,1:T(1,128)} %param.13) | copy-start | bytes 772
  31.7 48.1 %copy-start.5 = (f32[64]{0:T(128)S(1)}, f32[64]{0:T(128)}, u32[]{:S(2)}) copy-start(f32[64]{0:T(128)} %param.14) | copy-start | bytes 772
  31.7 1.8 %collective-permute-start.7 = (bf16[96,2048]{1,0:T(8,128)(2,1)S(1)}, bf16[96,2048]{1,0:T(8,128)(2,1)S(1)}, u32[]{:S(2)}, u32[]{:S(2)}) collective-permute-start(bf16[96,2048]{1,0:T(8,128)(2,1)S(1)} %get-tuple-element.8.own_ref), channel_id=1, source_target_pairs={{0,1},{1,0},{2,3},{3,2},{4,5},{5,4},{6,7},{7,6},{8,9},{9,8},{10,11... | collective-permute-start | bytes 1179656 | tf_op jit(solution)/shard_map/ppermute | solution.py:388
  39.5 40.2 %all-to-all-start.1 = ((bf16[16,24,640]{2,1,0:T(8,128)(2,1)}), bf16[16,24,640]{2,1,0:T(8,128)(2,1)S(1)}, u32[]{:S(2)}, u32[]{:S(2)}) async-start(bf16[16,24,640]{2,1,0:T(8,128)(2,1)} %down.1), calls=%async_computation.1 | async-start | bytes 983040 | tf_op jit(solution)/shard_map/all_to_all | solution.py:390
  45.6 8.8 %collective-permute-start = (bf16[64,512]{1,0:T(8,128)(2,1)S(1)}, bf16[64,512]{1,0:T(8,128)(2,1)S(1)}, u32[]{:S(2)}, u32[]{:S(2)}) collective-permute-start(bf16[64,512]{1,0:T(8,128)(2,1)S(1)} %get-tuple-element.6.refs_0_), channel_id=1, source_target_pairs={{0,8},{2,10},{4,12},{6,14},{8,16},{10,18},{12,20},{14,22},{16,24},... | collective-permute-start | bytes 196616 | tf_op jit(solution)/shard_map/ppermute | solution.py:370
  46.9 16.1 %collective-permute-start.1 = (bf16[64,512]{1,0:T(8,128)(2,1)S(1)}, bf16[64,512]{1,0:T(8,128)(2,1)S(1)}, u32[]{:S(2)}, u32[]{:S(2)}) collective-permute-start(bf16[64,512]{1,0:T(8,128)(2,1)S(1)} %get-tuple-element.6.refs_0_), channel_id=1, source_target_pairs={{0,16},{2,18},{4,20},{6,22},{8,24},{10,26},{12,28},{14,30},{1,17},... | collective-permute-start | bytes 196616 | tf_op jit(solution)/shard_map/ppermute | solution.py:370
  48.2 14.8 %collective-permute-start.2 = (bf16[64,512]{1,0:T(8,128)(2,1)S(1)}, bf16[64,512]{1,0:T(8,128)(2,1)S(1)}, u32[]{:S(2)}, u32[]{:S(2)}) collective-permute-start(bf16[64,512]{1,0:T(8,128)(2,1)S(1)} %get-tuple-element.6.refs_0_), channel_id=1, source_target_pairs={{0,24},{2,26},{4,28},{6,30},{1,25},{3,27},{5,29},{7,31}} | collective-permute-start | bytes 196616 | tf_op jit(solution)/shard_map/ppermute | solution.py:370
  62.9 9.2 %collective-permute-start.3 = (bf16[256,512]{1,0:T(8,128)(2,1)S(1)}, bf16[256,512]{1,0:T(8,128)(2,1)S(1)}, u32[]{:S(2)}, u32[]{:S(2)}) collective-permute-start(bf16[256,512]{1,0:T(8,128)(2,1)S(1)} %join.1.refs_0_), channel_id=1, source_target_pairs={{0,2},{2,0},{4,6},{6,4},{8,10},{10,8},{12,14},{14,12},{16,18},{18,... | collective-permute-start | bytes 786440 | tf_op jit(solution)/shard_map/ppermute | solution.py:374
  64.5 13.2 %collective-permute-start.4 = (bf16[256,512]{1,0:T(8,128)(2,1)S(1)}, bf16[256,512]{1,0:T(8,128)(2,1)S(1)}, u32[]{:S(2)}, u32[]{:S(2)}) collective-permute-start(bf16[256,512]{1,0:T(8,128)(2,1)S(1)} %join.1.refs_0_), channel_id=1, source_target_pairs={{0,4},{2,6},{4,0},{6,2},{8,12},{10,14},{12,8},{14,10},{16,20},{18,... | collective-permute-start | bytes 786440 | tf_op jit(solution)/shard_map/ppermute | solution.py:374
  65.0 12.7 %collective-permute-start.5 = (bf16[256,512]{1,0:T(8,128)(2,1)S(1)}, bf16[256,512]{1,0:T(8,128)(2,1)S(1)}, u32[]{:S(2)}, u32[]{:S(2)}) collective-permute-start(bf16[256,512]{1,0:T(8,128)(2,1)S(1)} %join.1.refs_0_), channel_id=1, source_target_pairs={{0,6},{2,4},{4,2},{6,0},{8,14},{10,12},{12,10},{14,8},{16,22},{18,... | collective-permute-start | bytes 786440 | tf_op jit(solution)/shard_map/ppermute | solution.py:374

commit v2 on v1

--- a/solution.py
+++ b/solution.py
@@ -15,6 +15,7 @@
 
 masked_score = -1e30
 COVER = int(2e10)
+lane = 128
 sublane = 8
 VMEM = pltpu.VMEM
 
@@ -46,15 +47,20 @@
     return jnp.sum(same, axis=0, keepdims=True)
 
 
-def pack_kernel(place_ref, side_ref, ids_ref, hidden_hbm, key_hbm, value_hbm, packed_ref, kv_ref, hidden_ref, sems, *, pieces):
+def pack_kernel(
+    place_ref, side_ref, ids_hbm, hidden_hbm, key_hbm, value_hbm, packed_ref, kv_ref, ids_ref, hidden_ref, sems, *, pieces
+):
     width_kv = key_hbm.shape[1]
     copies = [
         pltpu.make_async_copy(hidden_hbm, hidden_ref, sems.at[0]),
         pltpu.make_async_copy(key_hbm, kv_ref.at[:, pl.ds(0, width_kv)], sems.at[1]),
         pltpu.make_async_copy(value_hbm, kv_ref.at[:, pl.ds(width_kv, width_kv)], sems.at[2]),
     ]
+    ids_copy = pltpu.make_async_copy(ids_hbm, ids_ref, sems.at[3])
+    ids_copy.start()
     for copy in copies:
         copy.start()
+    ids_copy.wait()
     ids_row = ids_ref[...].astype(jnp.float32)
     rank = slots_of(ids_row)
     rows = EXPERTS * CAP * pieces
@@ -82,14 +88,17 @@
             VMEM((keys.shape[0], 2 * keys.shape[1]), jnp.bfloat16),
         ),
         in_specs=[pl.BlockSpec(memory_space=pltpu.SMEM)] * 2
-        + whole(1)
-        + [pl.BlockSpec(memory_space=pl.ANY)] * 3,
+        + [pl.BlockSpec(memory_space=pl.ANY)] * 4,
         out_specs=tuple(whole(2)),
-        scratch_shapes=[VMEM(hidden.shape, hidden.dtype), pltpu.SemaphoreType.DMA((3,))],
+        scratch_shapes=[
+            VMEM(ids_row.shape, ids_row.dtype),
+            VMEM(hidden.shape, hidden.dtype),
+            pltpu.SemaphoreType.DMA((4,)),
+        ],
         compiler_params=params(4),
         cost_estimate=pl.CostEstimate(flops=COVER, bytes_accessed=1, transcendentals=0),
         name="pack",
-    )(place, side, ids_row, far(hidden), far(keys), far(values))
+    )(place, side, far(ids_row), far(hidden), far(keys), far(values))
 
 
 def unpack_rows(arrived, pieces):
@@ -111,39 +120,44 @@
     return wide, width // wide
 
 
-def halves(own, rest, side):
-    return jnp.where(side == 0, own, rest), jnp.where(side == 0, rest, own)
-
-
 def early_rows(w_down):
-    return w_down.shape[1] * 3 // 4
-
-
-def gate_up_kernel(side_ref, own_ref, rest_ref, wg_ref, wu_ref, wd_hbm, inner_ref, wd_ref, sems, *, pieces):
+    return w_down.shape[1] * 7 // 8
+
+
+def gate_up_kernel(side_ref, own_ref, rest_ref, wg_ref, wu_ref, wd_hbm, inner_ref, wd_ref, x_ref, sems, *, pieces):
+    side = side_ref[0]
+    half = wd_hbm.shape[1] // 2
     early = wd_ref.shape[0]
-    parts = sems.shape[0]
-    copies = [
-        pltpu.make_async_copy(
-            wd_hbm.at[0, pl.ds(k * (early // parts), early // parts), :],
-            wd_ref.at[pl.ds(k * (early // parts), early // parts), :],
-            sems.at[k],
-        )
-        for k in range(parts)
-    ]
-    for copy in copies:
-        copy.start()
+
+    def fetch(k, place):
+        from_row, to_row, count = ((place * half, 0, half), ((1 - place) * half, half, early - half))[k]
+        return pltpu.make_async_copy(
+            wd_hbm.at[0, pl.ds(from_row, count), :], wd_ref.at[pl.ds(to_row, count), :], sems.at[k]
+        )
+
+    for place in range(2):
+
+        @pl.when(side == place)
+        def _():
+            for k in range(2):
+                fetch(k, place).start()
+
     rows = own_ref.shape[0] * own_ref.shape[1]
     width = own_ref.shape[2]
-    lo, hi = halves(own_ref[...].reshape(rows, width), rest_ref[...].reshape(rows, width), side_ref[0])
-    x = jnp.concatenate([unpack_rows(lo, pieces), unpack_rows(hi, pieces)], axis=1)
+    count = x_ref.shape[1] // 2
+    for ref, place in ((own_ref, side), (rest_ref, 1 - side)):
+        x_ref[:, pl.ds(pl.multiple_of(place * count, count), count)] = unpack_rows(
+            ref[...].reshape(rows, width), pieces
+        )
+    x = x_ref[...]
     wide, blocks = column_blocks(wg_ref.shape[2])
     for n in range(blocks):
         at = slice(n * wide, (n + 1) * wide)
         gate = jnp.dot(x, wg_ref[0, :, at], preferred_element_type=jnp.float32)
         up = jnp.dot(x, wu_ref[0, :, at], preferred_element_type=jnp.float32)
         inner_ref[:, at] = (gate / (1.0 + jnp.exp(-gate)) * up).astype(jnp.bfloat16)
-    for copy in copies:
-        copy.wait()
+    for k in range(2):
+        fetch(k, 0).wait()
 
 
 def gate_up(side, own, rest, wg, wu, wd, pieces):
@@ -159,8 +173,11 @@
         + whole(4)
         + [pl.BlockSpec(memory_space=pl.ANY)],
         out_specs=(near_spec, near_spec),
-        scratch_shapes=[pltpu.SemaphoreType.DMA((4,))],
-        compiler_params=params(6),
+        scratch_shapes=[
+            VMEM((rows, wg.shape[1]), jnp.bfloat16),
+            pltpu.SemaphoreType.DMA((2,)),
+        ],
+        compiler_params=params(4),
         cost_estimate=pl.CostEstimate(
             flops=4 * rows * wg.size, bytes_accessed=wd.size, transcendentals=0
         ),
@@ -168,35 +185,42 @@
     )(side, *near(own, rest, wg, wu), far(wd))
 
 
-def down_kernel(side_ref, own_ref, rest_ref, wd_ref, wd_hbm, out_ref, buf, sem, *, pieces):
+def down_kernel(side_ref, own_ref, rest_ref, wd_ref, wd_hbm, out_ref, buf, acc_ref, stack_ref, sem, *, pieces):
     early = wd_ref.shape[0]
-    copy = pltpu.make_async_copy(wd_hbm.at[0, pl.ds(early, buf.shape[0]), :], buf, sem)
-    copy.start()
-    lo, hi = halves(own_ref[...], rest_ref[...], side_ref[0])
-    x = jnp.concatenate([lo, hi], axis=1)
-    per = x.shape[0]
-    deep = math.gcd(early, buf.shape[0])
+    half = wd_hbm.shape[1] // 2
+
+    def fetch(place):
+        at = (1 - place) * half + early - half
+        return pltpu.make_async_copy(wd_hbm.at[0, pl.ds(at, buf.shape[0]), :], buf, sem)
+
+    for place in range(2):
+
+        @pl.when(side_ref[0] == place)
+        def _():
+            fetch(place).start()
+
+    per = own_ref.shape[0]
     wide, blocks = column_blocks(wd_ref.shape[1])
-
-    def partial(ref, first, n, total):
-        for k in range(ref.shape[0] // deep):
-            rows = slice(k * deep, (k + 1) * deep)
-            total = total + jnp.dot(
-                x[:, first + k * deep : first + (k + 1) * deep],
-                ref[rows, n * wide : (n + 1) * wide],
-                preferred_element_type=jnp.float32,
-            )
-        return total
-
-    zeros = jnp.zeros((per, wide), jnp.float32)
-    totals = [partial(wd_ref, 0, n, zeros) for n in range(blocks)]
-    copy.wait()
-    full = jnp.concatenate(
-        [partial(buf, early, n, totals[n]).astype(jnp.bfloat16) for n in range(blocks)], axis=1
-    )
-    width = full.shape[1] // pieces
-    rounded = [full[:, k * width : (k + 1) * width] for k in range(pieces)]
-    stacked = jnp.concatenate(rounded, axis=0)
+    for n in range(blocks):
+        at = slice(n * wide, (n + 1) * wide)
+        acc_ref[:, at] = jnp.dot(
+            own_ref[...], wd_ref[:half, at], preferred_element_type=jnp.float32
+        ) + jnp.dot(
+            rest_ref[:, : early - half], wd_ref[half:, at], preferred_element_type=jnp.float32
+        )
+    fetch(0).wait()
+    width = stack_ref.shape[1]
+    for n in range(blocks):
+        at = slice(n * wide, (n + 1) * wide)
+        total = acc_ref[:, at] + jnp.dot(
+            rest_ref[:, early - half :], buf[:, at], preferred_element_type=jnp.float32
+        )
+        rounded = total.astype(jnp.bfloat16)
+        for c in range(wide // lane):
+            piece, column = divmod(n * wide + c * lane, width)
+            stack_ref[piece * per : (piece + 1) * per, column : column + lane] = rounded[
+                :, c * lane : (c + 1) * lane
+            ]
     group = CAP * pieces
     rows = per * pieces
     number = lax.broadcasted_iota(jnp.int32, (rows, 1), 0)
@@ -205,7 +229,7 @@
     selector = jnp.where(
         lax.broadcasted_iota(jnp.int32, (rows, rows), 1) == wanted, 1.0, 0.0
     ).astype(jnp.bfloat16)
-    out = jnp.dot(selector, stacked, preferred_element_type=jnp.float32).astype(jnp.bfloat16)
+    out = jnp.dot(selector, stack_ref[...], preferred_element_type=jnp.float32).astype(jnp.bfloat16)
     out_ref[...] = out.reshape(out_ref.shape)
 
 
@@ -218,7 +242,12 @@
         + whole(3)
         + [pl.BlockSpec(memory_space=pl.ANY)],
         out_specs=pl.BlockSpec(memory_space=VMEM),
-        scratch_shapes=[VMEM((left, w.shape[2]), w.dtype), pltpu.SemaphoreType.DMA],
+        scratch_shapes=[
+            VMEM((left, w.shape[2]), w.dtype),
+            VMEM((own.shape[0], w.shape[2]), jnp.float32),
+            VMEM((own.shape[0] * pieces, w.shape[2] // pieces), jnp.bfloat16),
+            pltpu.SemaphoreType.DMA,
+        ],
         compiler_params=params(10),
         cost_estimate=pl.CostEstimate(
             flops=2 * own.shape[0] * w.size, bytes_accessed=w.size, transcendentals=0
@@ -258,22 +287,22 @@
     )(*near(ids_row, gain_row, back))
 
 
-def join_kernel(*refs):
-    rows = refs[0].shape[0]
-    for k, ref in enumerate(refs[:-1]):
-        refs[-1][k * rows : (k + 1) * rows, :] = ref[...]
-
-
-def join(parts):
-    rows, width = parts[0].shape
+def join_kernel(*refs, count):
+    first = 0
+    for ref in refs[:count]:
+        refs[-1][first : first + ref.shape[0], :] = ref[...]
+        first += ref.shape[0]
+
+
+def join(parts, after=()):
     return pl.pallas_call(
-        join_kernel,
-        out_shape=VMEM((len(parts) * rows, width), parts[0].dtype),
-        in_specs=whole(len(parts)),
+        functools.partial(join_kernel, count=len(parts)),
+        out_shape=VMEM((sum(p.shape[0] for p in parts), parts[0].shape[1]), parts[0].dtype),
+        in_specs=whole(len(parts)) + [pl.BlockSpec(memory_space=pl.ANY)] * len(after),
         out_specs=pl.BlockSpec(memory_space=VMEM),
-        compiler_params=params(),
+        compiler_params=params(2),
         name="join",
-    )(*near(*parts))
+    )(*near(*parts), *after)
 
 
 def attend_kernel(place_ref, query_ref, *refs, owner_of):
@@ -359,28 +388,19 @@
     gain_row = route_gain.reshape(1, -1)
 
     packed, kv = pack(place, side, ids_row, hidden, projected_keys, projected_values, pieces)
-    if hosts > 1:
-        packed = jnp.repeat(packed, hosts, axis=0)
+    beside = lax.ppermute(kv, "ctx", [(i, i ^ plane) for i in range(ctx_count)])
     arrived = lax.all_to_all(packed, "ctx", split_axis=0, concat_axis=0, tiled=True)
-
-    if hosts == 1:
-        slabs = [kv]
-        for step in range(1, ctx_count // plane):
-            pairs = [(i, i + step * plane) for i in range(ctx_count - step * plane)]
-            slabs.append(lax.ppermute(kv, "ctx", pairs))
-        column = join(slabs)
-        parts = [column]
-        for flip in range(1, plane):
-            parts.append(lax.ppermute(column, "ctx", [(i, i ^ flip) for i in range(ctx_count)]))
-
-        def owner_of(me, part, block):
-            layer = lax.div(me, plane) - block
-            return layer * plane + (lax.rem(me, plane) ^ part), layer >= 0
-    else:
-        parts = [lax.all_gather(kv, "ctx", axis=0, tiled=True)]
-
-        def owner_of(me, part, block):
-            return block, block >= 0
+    pair = join([kv, beside], (arrived,))
+    below = lax.ppermute(pair, "ctx", [(i, i + 2 * plane) for i in range(ctx_count - 2 * plane)])
+    column = join([pair, below])
+    parts = [column]
+    for flip in range(1, plane):
+        parts.append(lax.ppermute(column, "ctx", [(i, i ^ flip) for i in range(ctx_count)]))
+
+    def owner_of(me, part, block):
+        layer = lax.div(me, plane)
+        held = jnp.logical_or(block < 2, layer >= 2)
+        return (layer ^ block) * plane + (lax.rem(me, plane) ^ part), held
 
     other = [(0, 1), (1, 0)]
     arrived_rest = lax.ppermute(arrived, "tp", other)

time: 81.5 us -> 81.1 us (level)
  the two profiles are of different devices: /device:TPU:28 before, /device:TPU:0 now
where the time goes in v2:
time: 81.1 us; the launch traced here: 80.9 us
  waiting for transfers between devices  24.6 us (30%)
  blocking collectives  22.9 us (28%)
  Pallas kernels  18 us (22%)
  starting transfers between devices  14.6 us (18%)
    all_to_all x1, blocking collectives, body(): lax.all_to_all(packed, 'ctx', split_axis=0, concat_axis=0, tiled=True)  22.9 us
    ppermute x3, waiting for transfers between devices, body(): lax.ppermute(column, 'ctx', [(i, i ^ flip) for i in range(ctx_count)])  9.44 us
    ppermute x1, waiting for transfers between devices, body(): beside = lax.ppermute(kv, 'ctx', [(i, i ^ plane) for i in range(ctx_count)])  9.24 us
    pallas_call x1, Pallas kernels, gate_up(): pl.pallas_call(functools.partial(gate_up_kernel, pieces=pieces), out_shap...  7.78 us
    pallas_call x1, Pallas kernels, down(): pl.pallas_call(functools.partial(down_kernel, pieces=pieces), out_shape=V...  5.26 us
    ppermute x1, starting transfers between devices, body(): lax.ppermute(pair, 'ctx', [(i, i + 2 * plane) for i in range(ctx_count -...  5.01 us
    all_to_all x1, starting transfers between devices, body(): lax.all_to_all(result, 'ctx', split_axis=0, concat_axis=0, tiled=True)  3.85 us
    ppermute x3, starting transfers between devices, body(): lax.ppermute(column, 'ctx', [(i, i ^ flip) for i in range(ctx_count)])  3.55 us
  transfers between devices with their start and end apart: 8, of which 6 were waited for; matrix products, arithmetic and copies ran while one was open for 0% of the time, Pallas kernels for 3%

profile of v2, /device:TPU:0, one launch (start us, length us, event | category | flops | bytes accessed | tf_op | source)
XLA Modules:
  0.0 80.9 jit_solution(13390980031348258312)
XLA Ops:
  0.6 0.0 copy-start
  0.6 0.0 copy-start.1
  0.7 1.5 %pack.1 = (bf16[16,24,640]{2,1,0:T(8,128)(2,1)S(1)}, bf16[64,512]{1,0:T(8,128)(2,1)S(1)}) custom-call(s32[1]{0:T(128)} %bitcast.place_ref, s32[1]{0:T(128)} %bitcast.1.side_ref, s32[1,64]{1,0:T(1,128)} %bitcast.6, bf16[64,2560]{1,0:T(8,128)(2,1)} %hidden_hbm.1, bf16[64,256]{1,0:T(8,128)(2,1)} %key_hbm.1, bf16[64,256]{1,0:T(8,128)(2,1)} %value_hbm.1), custom_call_target="tpu_custom_call" | custom-call | flops 20000000000 | bytes 1 | tf_op jit(solution)/shard_map/pack/pallas_call | solution.py:84
  2.2 22.9 %all_to_all.10.refs_2_.own_ref = bf16[16,24,640]{2,1,0:T(8,128)(2,1)S(1)} all-to-all(bf16[16,24,640]{2,1,0:T(8,128)(2,1)S(1)} %get-tuple-element.7), channel_id=1, replica_groups=mesh['ctx'=16,'tp'=2] {'ctx'}, dimensions={0} | all-to-all | bytes 983040 | tf_op jit(solution)/shard_map/all_to_all | solution.py:392
  25.1 0.0 collective-permute-start.5
  25.1 1.9 %collective-permute-done.5.rest_ref = bf16[16,24,640]{2,1,0:T(8,128)(2,1)S(1)} collective-permute-done((bf16[16,24,640]{2,1,0:T(8,128)(2,1)S(1)}, bf16[16,24,640]{2,1,0:T(8,128)(2,1)S(1)}, u32[]{:S(2)}, u32[]{:S(2)}) %collective-permute-start.5) | collective-permute-done | bytes 491552 | tf_op jit(solution)/shard_map/ppermute | solution.py:406
  26.9 0.0 copy-done
  26.9 0.0 copy-done.1
  26.9 7.8 %gate_up.1 = (bf16[96,2048]{1,0:T(8,128)(2,1)S(1)}, bf16[3584,2560]{1,0:T(8,128)(2,1)S(1)}) custom-call(s32[1]{0:T(128)} %bitcast.1.side_ref, bf16[16,24,640]{2,1,0:T(8,128)(2,1)S(1)} %all_to_all.10.refs_2_.own_ref, bf16[16,24,640]{2,1,0:T(8,128)(2,1)S(1)} %collective-permute-done.5.rest_ref, bf16[1,5120,2048]{2,1,0:T(8,128)(2,1)S(1)} %copy-done, ...), custom_call_target="tpu_custom_call" | custom-call | flops 4026531840 | bytes 10485760 | tf_op jit(solution)/shard_map/gate_up/pallas_call | solution.py:166
  34.7 0.2 collective-permute-start.6
  34.9 1.6 %collective-permute-done.6.rest_ref = bf16[96,2048]{1,0:T(8,128)(2,1)S(1)} collective-permute-done((bf16[96,2048]{1,0:T(8,128)(2,1)S(1)}, bf16[96,2048]{1,0:T(8,128)(2,1)S(1)}, u32[]{:S(2)}, u32[]{:S(2)}) %collective-permute-start.6) | collective-permute-done | bytes 393248 | tf_op jit(solution)/shard_map/ppermute | solution.py:408
  36.5 0.0 copy-start.2
  36.5 0.0 copy-start.3
  36.5 0.0 copy-start.4
  36.5 5.3 %down.1 = bf16[16,24,640]{2,1,0:T(8,128)(2,1)} custom-call(s32[1]{0:T(128)} %bitcast.1.side_ref, bf16[96,2048]{1,0:T(8,128)(2,1)S(1)} %get-tuple-element.8.own_ref, bf16[96,2048]{1,0:T(8,128)(2,1)S(1)} %collective-permute-done.6.rest_ref, bf16[3584,2560]{1,0:T(8,128)(2,1)S(1)} %get-tuple-element.9.wd_ref, bf16[1,4096,2560]{2,1,0:T(8,128)(2,1)} %wd_hbm.3), custom_call_target="tpu_custom_call" | custom-call | flops 2013265920 | bytes 10485760 | tf_op jit(solution)/shard_map/down/pallas_call | solution.py:238
  41.8 3.8 %all-to-all-start.1 = ((bf16[16,24,640]{2,1,0:T(8,128)(2,1)}), bf16[16,24,640]{2,1,0:T(8,128)(2,1)S(1)}, u32[]{:S(2)}, u32[]{:S(2)}) async-start(bf16[16,24,640]{2,1,0:T(8,128)(2,1)} %down.1), calls=%async_computation.1 | async-start | bytes 983040 | tf_op jit(solution)/shard_map/all_to_all | solution.py:410
  45.6 1.9 %collective-permute-start = (bf16[64,512]{1,0:T(8,128)(2,1)S(1)}, bf16[64,512]{1,0:T(8,128)(2,1)S(1)}, u32[]{:S(2)}, u32[]{:S(2)}) collective-permute-start(bf16[64,512]{1,0:T(8,128)(2,1)S(1)} %get-tuple-element.6.refs_0_), channel_id=1, source_target_pairs={{0,8},{2,10},{4,12},{6,14},{8,0},{10,2},{12,4},{14,6},{16,24},{18,... | collective-permute-start | bytes 196616 | tf_op jit(solution)/shard_map/ppermute | solution.py:391
  47.6 9.2 %collective-permute-done.refs_1_ = bf16[64,512]{1,0:T(8,128)(2,1)S(1)} collective-permute-done((bf16[64,512]{1,0:T(8,128)(2,1)S(1)}, bf16[64,512]{1,0:T(8,128)(2,1)S(1)}, u32[]{:S(2)}, u32[]{:S(2)}) %collective-permute-start) | collective-permute-done | bytes 65568 | tf_op jit(solution)/shard_map/ppermute | solution.py:391
  56.8 5.0 %collective-permute-start.1 = (bf16[128,512]{1,0:T(8,128)(2,1)S(1)}, bf16[128,512]{1,0:T(8,128)(2,1)S(1)}, u32[]{:S(2)}, u32[]{:S(2)}) collective-permute-start(bf16[128,512]{1,0:T(8,128)(2,1)S(1)} %join.2.refs_0_), channel_id=1, source_target_pairs={{0,16},{2,18},{4,20},{6,22},{8,24},{10,26},{12,28},{14,30},{1,17},... | collective-permute-start | bytes 393224 | tf_op jit(solution)/shard_map/ppermute | solution.py:394
  61.8 2.5 %collective-permute-done.1.refs_1_ = bf16[128,512]{1,0:T(8,128)(2,1)S(1)} collective-permute-done((bf16[128,512]{1,0:T(8,128)(2,1)S(1)}, bf16[128,512]{1,0:T(8,128)(2,1)S(1)}, u32[]{:S(2)}, u32[]{:S(2)}) %collective-permute-start.1) | collective-permute-done | bytes 131104 | tf_op jit(solution)/shard_map/ppermute | solution.py:394
  64.4 2.4 %collective-permute-start.4 = (bf16[256,512]{1,0:T(8,128)(2,1)S(1)}, bf16[256,512]{1,0:T(8,128)(2,1)S(1)}, u32[]{:S(2)}, u32[]{:S(2)}) collective-permute-start(bf16[256,512]{1,0:T(8,128)(2,1)S(1)} %join.3.refs_0_), channel_id=1, source_target_pairs={{0,6},{2,4},{4,2},{6,0},{8,14},{10,12},{12,10},{14,8},{16,22},{18,... | collective-permute-start | bytes 786440 | tf_op jit(solution)/shard_map/ppermute | solution.py:398
  66.8 0.6 collective-permute-start.3
  67.4 0.6 collective-permute-start.2
  67.9 6.6 %collective-permute-done.4.refs_3_ = bf16[256,512]{1,0:T(8,128)(2,1)S(1)} collective-permute-done((bf16[256,512]{1,0:T(8,128)(2,1)S(1)}, bf16[256,512]{1,0:T(8,128)(2,1)S(1)}, u32[]{:S(2)}, u32[]{:S(2)}) %collective-permute-start.4) | collective-permute-done | bytes 262176 | tf_op jit(solution)/shard_map/ppermute | solution.py:398
  74.5 2.8 %collective-permute-done.3.refs_2_ = bf16[256,512]{1,0:T(8,128)(2,1)S(1)} collective-permute-done((bf16[256,512]{1,0:T(8,128)(2,1)S(1)}, bf16[256,512]{1,0:T(8,128)(2,1)S(1)}, u32[]{:S(2)}, u32[]{:S(2)}) %collective-permute-start.3) | collective-permute-done | bytes 262176 | tf_op jit(solution)/shard_map/ppermute | solution.py:398
  77.4 0.0 collective-permute-done.2.refs_1_
  77.4 0.0 copy-done.2
  77.4 2.1 %attend.1 = bf16[64,1280]{1,0:T(8,128)(2,1)} custom-call(s32[1]{0:T(128)} %bitcast.place_ref, bf16[64,1280]{1,0:T(8,128)(2,1)S(1)} %copy-done.2, bf16[256,512]{1,0:T(8,128)(2,1)S(1)} %join.3.refs_0_, bf16[256,512]{1,0:T(8,128)(2,1)S(1)} %collective-permute-done.2.refs_1_, bf16[256,512]{1,0:T(8,128)(2,1)S(1)} %collective-permute-done.3.refs_2_, ...), custom_call_target="tpu_custom_call" | custom-call | tf_op jit(solution)/shard_map/attend/pallas_call | solution.py:366
  79.4 0.0 all-to-all-done.1
  79.4 0.0 copy-done.3
  79.4 0.0 copy-done.4
  79.4 1.4 %combine.1 = bf16[64,2560]{1,0:T(8,128)(2,1)} custom-call(s32[1,64]{1,0:T(1,128)S(1)} %bitcast.7, f32[1,64]{1,0:T(1,128)S(1)} %bitcast.8, bf16[1,16,24,640]{3,2,1,0:T(8,128)(2,1)S(1)} %bitcast.5), custom_call_target="tpu_custom_call" | custom-call | tf_op jit(solution)/shard_map/combine/pallas_call | solution.py:280
  (2 shorter events, 0.0 us)
Async XLA Ops:
  0.6 26.3 %copy-start = (bf16[1,5120,2048]{2,1,0:T(8,128)(2,1)S(1)}, bf16[1,5120,2048]{2,1,0:T(8,128)(2,1)}, u32[]{:S(2)}) copy-start(bf16[1,5120,2048]{2,1,0:T(8,128)(2,1)} %wg_ref.1) | copy-start | bytes 62914564
  0.6 26.3 %copy-start.1 = (bf16[1,5120,2048]{2,1,0:T(8,128)(2,1)S(1)}, bf16[1,5120,2048]{2,1,0:T(8,128)(2,1)}, u32[]{:S(2)}) copy-start(bf16[1,5120,2048]{2,1,0:T(8,128)(2,1)} %wu_ref.1) | copy-start | bytes 62914564
  25.1 1.9 %collective-permute-start.5 = (bf16[16,24,640]{2,1,0:T(8,128)(2,1)S(1)}, bf16[16,24,640]{2,1,0:T(8,128)(2,1)S(1)}, u32[]{:S(2)}, u32[]{:S(2)}) collective-permute-start(bf16[16,24,640]{2,1,0:T(8,128)(2,1)S(1)} %all_to_all.10.refs_2_.own_ref), channel_id=1, source_target_pairs={{0,1},{1,0},{2,3},{3,2},{4,5},{5,4},{6,7},{7,6},{8,9},{9,8},{10,11... | collective-permute-start | bytes 1474568 | tf_op jit(solution)/shard_map/ppermute | solution.py:406
  34.7 1.8 %collective-permute-start.6 = (bf16[96,2048]{1,0:T(8,128)(2,1)S(1)}, bf16[96,2048]{1,0:T(8,128)(2,1)S(1)}, u32[]{:S(2)}, u32[]{:S(2)}) collective-permute-start(bf16[96,2048]{1,0:T(8,128)(2,1)S(1)} %get-tuple-element.8.own_ref), channel_id=1, source_target_pairs={{0,1},{1,0},{2,3},{3,2},{4,5},{5,4},{6,7},{7,6},{8,9},{9,8},{10,11... | collective-permute-start | bytes 1179656 | tf_op jit(solution)/shard_map/ppermute | solution.py:408
  36.5 40.8 %copy-start.2 = (bf16[64,1280]{1,0:T(8,128)(2,1)S(1)}, bf16[64,1280]{1,0:T(8,128)(2,1)}, u32[]{:S(2)}) copy-start(bf16[64,1280]{1,0:T(8,128)(2,1)} %query_ref.1) | copy-start | bytes 491524
  36.5 42.9 %copy-start.3 = (s32[64,1]{0,1:T(1,128)S(1)}, s32[64,1]{0,1:T(1,128)}, u32[]{:S(2)}) copy-start(s32[64,1]{0,1:T(1,128)} %param.13) | copy-start | bytes 772
  36.5 42.9 %copy-start.4 = (f32[64]{0:T(128)S(1)}, f32[64]{0:T(128)}, u32[]{:S(2)}) copy-start(f32[64]{0:T(128)} %param.14) | copy-start | bytes 772
  41.8 37.6 %all-to-all-start.1 = ((bf16[16,24,640]{2,1,0:T(8,128)(2,1)}), bf16[16,24,640]{2,1,0:T(8,128)(2,1)S(1)}, u32[]{:S(2)}, u32[]{:S(2)}) async-start(bf16[16,24,640]{2,1,0:T(8,128)(2,1)} %down.1), calls=%async_computation.1 | async-start | bytes 983040 | tf_op jit(solution)/shard_map/all_to_all | solution.py:410
  45.6 11.2 %collective-permute-start = (bf16[64,512]{1,0:T(8,128)(2,1)S(1)}, bf16[64,512]{1,0:T(8,128)(2,1)S(1)}, u32[]{:S(2)}, u32[]{:S(2)}) collective-permute-start(bf16[64,512]{1,0:T(8,128)(2,1)S(1)} %get-tuple-element.6.refs_0_), channel_id=1, source_target_pairs={{0,8},{2,10},{4,12},{6,14},{8,0},{10,2},{12,4},{14,6},{16,24},{18,... | collective-permute-start | bytes 196616 | tf_op jit(solution)/shard_map/ppermute | solution.py:391
  56.8 7.5 %collective-permute-start.1 = (bf16[128,512]{1,0:T(8,128)(2,1)S(1)}, bf16[128,512]{1,0:T(8,128)(2,1)S(1)}, u32[]{:S(2)}, u32[]{:S(2)}) collective-permute-start(bf16[128,512]{1,0:T(8,128)(2,1)S(1)} %join.2.refs_0_), channel_id=1, source_target_pairs={{0,16},{2,18},{4,20},{6,22},{8,24},{10,26},{12,28},{14,30},{1,17},... | collective-permute-start | bytes 393224 | tf_op jit(solution)/shard_map/ppermute | solution.py:394
  64.4 10.2 %collective-permute-start.4 = (bf16[256,512]{1,0:T(8,128)(2,1)S(1)}, bf16[256,512]{1,0:T(8,128)(2,1)S(1)}, u32[]{:S(2)}, u32[]{:S(2)}) collective-permute-start(bf16[256,512]{1,0:T(8,128)(2,1)S(1)} %join.3.refs_0_), channel_id=1, source_target_pairs={{0,6},{2,4},{4,2},{6,0},{8,14},{10,12},{12,10},{14,8},{16,22},{18,... | collective-permute-start | bytes 786440 | tf_op jit(solution)/shard_map/ppermute | solution.py:398
  66.8 10.6 %collective-permute-start.3 = (bf16[256,512]{1,0:T(8,128)(2,1)S(1)}, bf16[256,512]{1,0:T(8,128)(2,1)S(1)}, u32[]{:S(2)}, u32[]{:S(2)}) collective-permute-start(bf16[256,512]{1,0:T(8,128)(2,1)S(1)} %join.3.refs_0_), channel_id=1, source_target_pairs={{0,4},{2,6},{4,0},{6,2},{8,12},{10,14},{12,8},{14,10},{16,20},{18,... | collective-permute-start | bytes 786440 | tf_op jit(solution)/shard_map/ppermute | solution.py:398
  67.4 10.0 %collective-permute-start.2 = (bf16[256,512]{1,0:T(8,128)(2,1)S(1)}, bf16[256,512]{1,0:T(8,128)(2,1)S(1)}, u32[]{:S(2)}, u32[]{:S(2)}) collective-permute-start(bf16[256,512]{1,0:T(8,128)(2,1)S(1)} %join.3.refs_0_), channel_id=1, source_target_pairs={{0,2},{2,0},{4,6},{6,4},{8,10},{10,8},{12,14},{14,12},{16,18},{18,... | collective-permute-start | bytes 786440 | tf_op jit(solution)/shard_map/ppermute | solution.py:398

commit v3 on v2

--- a/solution.py
+++ b/solution.py
@@ -185,7 +185,9 @@
     )(side, *near(own, rest, wg, wu), far(wd))
 
 
-def down_kernel(side_ref, own_ref, rest_ref, wd_ref, wd_hbm, out_ref, buf, acc_ref, stack_ref, sem, *, pieces):
+def down_kernel(
+    side_ref, own_ref, rest_ref, wd_ref, wd_hbm, out_hbm, out_ref, buf, acc_ref, stack_ref, sem, out_sems, *, pieces
+):
     early = wd_ref.shape[0]
     half = wd_hbm.shape[1] // 2
 
@@ -226,27 +228,42 @@
     number = lax.broadcasted_iota(jnp.int32, (rows, 1), 0)
     source, left = number // group, number % group
     wanted = (left // CAP) * per + source * CAP + left % CAP
-    selector = jnp.where(
-        lax.broadcasted_iota(jnp.int32, (rows, rows), 1) == wanted, 1.0, 0.0
-    ).astype(jnp.bfloat16)
-    out = jnp.dot(selector, stack_ref[...], preferred_element_type=jnp.float32).astype(jnp.bfloat16)
-    out_ref[...] = out.reshape(out_ref.shape)
+    parts = out_sems.shape[0]
+    count = rows // parts
+    sources = out_hbm.shape[0] // parts
+    copies = []
+    for p in range(parts):
+        at = slice(p * count, (p + 1) * count)
+        selector = jnp.where(
+            lax.broadcasted_iota(jnp.int32, (count, rows), 1) == wanted[at], 1.0, 0.0
+        ).astype(jnp.bfloat16)
+        out = jnp.dot(selector, stack_ref[...], preferred_element_type=jnp.float32)
+        blocks_at = slice(p * sources, (p + 1) * sources)
+        out_ref[blocks_at] = out.astype(jnp.bfloat16).reshape((sources,) + out_ref.shape[1:])
+        copies.append(
+            pltpu.make_async_copy(out_ref.at[blocks_at], out_hbm.at[blocks_at], out_sems.at[p])
+        )
+        copies[-1].start()
+    for done in copies:
+        done.wait()
 
 
 def down(side, own, rest, early, w, sources, pieces):
     left = w.shape[1] - early.shape[0]
     return pl.pallas_call(
         functools.partial(down_kernel, pieces=pieces),
-        out_shape=VMEM((sources, CAP * pieces, w.shape[2] // pieces), jnp.bfloat16),
+        out_shape=pltpu.HBM((sources, CAP * pieces, w.shape[2] // pieces), jnp.bfloat16),
         in_specs=[pl.BlockSpec(memory_space=pltpu.SMEM)]
         + whole(3)
         + [pl.BlockSpec(memory_space=pl.ANY)],
-        out_specs=pl.BlockSpec(memory_space=VMEM),
+        out_specs=pl.BlockSpec(memory_space=pl.ANY),
         scratch_shapes=[
+            VMEM((sources, CAP * pieces, w.shape[2] // pieces), jnp.bfloat16),
             VMEM((left, w.shape[2]), w.dtype),
             VMEM((own.shape[0], w.shape[2]), jnp.float32),
             VMEM((own.shape[0] * pieces, w.shape[2] // pieces), jnp.bfloat16),
             pltpu.SemaphoreType.DMA,
+            pltpu.SemaphoreType.DMA((2,)),
         ],
         compiler_params=params(10),
         cost_estimate=pl.CostEstimate(
@@ -256,35 +273,46 @@
     )(side, *near(own, rest, early), far(w))
 
 
-def combine_kernel(ids_ref, gain_ref, back_ref, mixed_ref, *, pieces, hosts):
+def route_columns(ids_ref, gain_ref, route_ref, pieces):
     ids_row = ids_ref[...].astype(jnp.float32)
-    count = ids_row.shape[1]
-    rank = slots_of(ids_row)
-    width = back_ref.shape[3]
-    group = CAP * pieces
-    slot = ids_row * group + rank
-    gain = jnp.broadcast_to(gain_ref[...], (sublane, count)).T[:, 0:1]
-    first = jnp.broadcast_to(slot, (sublane, count)).T[:, 0:1]
-    column = lax.broadcasted_iota(jnp.int32, (count, EXPERTS * group), 1).astype(jnp.float32)
+    slot = ids_row * (CAP * pieces) + slots_of(ids_row)
+    route_ref[:, :lane] = jnp.broadcast_to(slot, (lane, slot.shape[1])).T
+    route_ref[:, lane:] = jnp.broadcast_to(gain_ref[...], (lane, slot.shape[1])).T
+
+
+def combine_kernel(route_ref, back_ref, mixed_hbm, mixed_ref, sems, *, pieces):
+    count = route_ref.shape[0]
+    experts, group, width = back_ref.shape
+    back = back_ref[...].reshape(experts * group, width)
+    slot = route_ref[:, 0:1]
+    gain = route_ref[:, lane : lane + 1]
+    column = lax.broadcasted_iota(jnp.int32, (count, experts * group), 1).astype(jnp.float32)
+    copies = []
     for k in range(pieces):
-        selector = jnp.where(column == first + float(k * CAP), 1.0, 0.0).astype(jnp.bfloat16)
-        picked = jnp.zeros((count, width), jnp.float32)
-        for h in range(hosts):
-            piece_rows = back_ref[h].reshape(EXPERTS * group, width)
-            picked = picked + jnp.dot(selector, piece_rows, preferred_element_type=jnp.float32)
-        mixed_ref[:, k * width : (k + 1) * width] = (picked * gain).astype(jnp.bfloat16)
-
-
-def combine(ids_row, gain_row, back, pieces):
-    hosts, _, _, width = back.shape
+        selector = jnp.where(column == slot + float(k * CAP), 1.0, 0.0).astype(jnp.bfloat16)
+        picked = jnp.dot(selector, back, preferred_element_type=jnp.float32)
+        at = slice(k * width, (k + 1) * width)
+        mixed_ref[:, at] = (picked * gain).astype(jnp.bfloat16)
+        copies.append(pltpu.make_async_copy(mixed_ref.at[:, at], mixed_hbm.at[:, at], sems.at[k]))
+        copies[-1].start()
+    for copy in copies:
+        copy.wait()
+
+
+def combine(route, back, pieces):
+    count, width = route.shape[0], back.shape[2] * pieces
     return pl.pallas_call(
-        functools.partial(combine_kernel, pieces=pieces, hosts=hosts),
-        out_shape=jax.ShapeDtypeStruct((ids_row.shape[1], width * pieces), jnp.bfloat16),
-        in_specs=whole(3),
-        out_specs=pl.BlockSpec(memory_space=VMEM),
-        compiler_params=params(),
+        functools.partial(combine_kernel, pieces=pieces),
+        out_shape=pltpu.HBM((count, width), jnp.bfloat16),
+        in_specs=whole(2),
+        out_specs=pl.BlockSpec(memory_space=pl.ANY),
+        scratch_shapes=[
+            VMEM((count, width), jnp.bfloat16),
+            pltpu.SemaphoreType.DMA((pieces,)),
+        ],
+        compiler_params=params(4),
         name="combine",
-    )(*near(ids_row, gain_row, back))
+    )(*near(route, back))
 
 
 def join_kernel(*refs, count):
@@ -305,9 +333,10 @@
     )(*near(*parts), *after)
 
 
-def attend_kernel(place_ref, query_ref, *refs, owner_of):
-    out_ref = refs[-1]
-    parts = refs[:-1]
+def attend_kernel(place_ref, ids_ref, gain_ref, query_ref, *refs, owner_of, pieces):
+    out_ref, route_ref = refs[-2:]
+    parts = refs[:-2]
+    route_columns(ids_ref, gain_ref, route_ref, pieces)
     tok = query_ref.shape[0]
     kv_width = parts[0].shape[1] // 2
     kv_heads = kv_width // HEAD_SIZE
@@ -362,15 +391,18 @@
             ]
 
 
-def attend(place, queries, parts, owner_of):
+def attend(place, ids_row, gain_row, queries, parts, owner_of, pieces):
     return pl.pallas_call(
-        functools.partial(attend_kernel, owner_of=owner_of),
-        out_shape=jax.ShapeDtypeStruct(queries.shape, jnp.bfloat16),
-        in_specs=[pl.BlockSpec(memory_space=pltpu.SMEM)] + whole(1 + len(parts)),
-        out_specs=pl.BlockSpec(memory_space=VMEM),
+        functools.partial(attend_kernel, owner_of=owner_of, pieces=pieces),
+        out_shape=(
+            jax.ShapeDtypeStruct(queries.shape, jnp.bfloat16),
+            VMEM((queries.shape[0], 2 * lane), jnp.float32),
+        ),
+        in_specs=[pl.BlockSpec(memory_space=pltpu.SMEM)] + whole(3 + len(parts)),
+        out_specs=tuple(whole(2)),
         compiler_params=params(8 + 40 * sum(p.shape[0] for p in parts) // 8192),
         name="attend",
-    )(place, *near(queries, *parts))
+    )(place, *near(ids_row, gain_row, queries, *parts))
 
 
 plane = 4
@@ -382,7 +414,6 @@
     ctx_count = lax.axis_size("ctx")
     place = lax.axis_index("ctx").astype(jnp.int32).reshape(1)
     side = lax.axis_index("tp").astype(jnp.int32).reshape(1)
-    hosts = ctx_count // EXPERTS
     pieces = sublane // math.gcd(CAP, sublane)
     ids_row = route_ids.reshape(1, -1)
     gain_row = route_gain.reshape(1, -1)
@@ -408,9 +439,8 @@
     inner_rest = lax.ppermute(inner, "tp", other)
     result = down(side, inner, inner_rest, early, w_down, ctx_count, pieces)
     back = lax.all_to_all(result, "ctx", split_axis=0, concat_axis=0, tiled=True)
-    attended = attend(place, queries, parts, owner_of)
-    back = back.reshape(EXPERTS, hosts, CAP * pieces, -1).transpose(1, 0, 2, 3)
-    mixed = combine(ids_row, gain_row, back, pieces)
+    attended, route = attend(place, ids_row, gain_row, queries, parts, owner_of, pieces)
+    mixed = combine(route, back, pieces)
     return (attended, mixed)
 
 

time: 81.1 us -> 80.3 us (level)
  no operation moved by 1% of the time
where the time goes in v3:
time: 80.3 us; the launch traced here: 80.1 us
  waiting for transfers between devices  24.6 us (31%)
  blocking collectives  22.9 us (29%)
  Pallas kernels  17.3 us (22%)
  starting transfers between devices  14.6 us (18%)
    all_to_all x1, blocking collectives, body(): lax.all_to_all(packed, 'ctx', split_axis=0, concat_axis=0, tiled=True)  22.9 us
    ppermute x3, waiting for transfers between devices, body(): lax.ppermute(column, 'ctx', [(i, i ^ flip) for i in range(ctx_count)])  9.44 us
    ppermute x1, waiting for transfers between devices, body(): beside = lax.ppermute(kv, 'ctx', [(i, i ^ plane) for i in range(ctx_count)])  9.24 us
    pallas_call x1, Pallas kernels, gate_up(): pl.pallas_call(functools.partial(gate_up_kernel, pieces=pieces), out_shap...  7.78 us
    ppermute x1, starting transfers between devices, body(): lax.ppermute(pair, 'ctx', [(i, i + 2 * plane) for i in range(ctx_count -...  5.01 us
    pallas_call x1, Pallas kernels, down(): pl.pallas_call(functools.partial(down_kernel, pieces=pieces), out_shape=p...  4.7 us
    all_to_all x1, starting transfers between devices, body(): lax.all_to_all(result, 'ctx', split_axis=0, concat_axis=0, tiled=True)  3.85 us
    ppermute x3, starting transfers between devices, body(): lax.ppermute(column, 'ctx', [(i, i ^ flip) for i in range(ctx_count)])  3.55 us
  transfers between devices with their start and end apart: 8, of which 6 were waited for; matrix products, arithmetic and copies ran while one was open for 0% of the time, Pallas kernels for 3%

profile of v3, /device:TPU:0, one launch (start us, length us, event | category | flops | bytes accessed | tf_op | source)
XLA Modules:
  0.0 80.1 jit_solution(17560116175640680216)
XLA Ops:
  0.6 0.0 copy-start
  0.6 0.0 copy-start.1
  0.7 1.5 %pack.1 = (bf16[16,24,640]{2,1,0:T(8,128)(2,1)S(1)}, bf16[64,512]{1,0:T(8,128)(2,1)S(1)}) custom-call(s32[1]{0:T(128)} %bitcast.place_ref, s32[1]{0:T(128)} %bitcast.3.side_ref, s32[1,64]{1,0:T(1,128)} %bitcast.4, bf16[64,2560]{1,0:T(8,128)(2,1)} %hidden_hbm.1, bf16[64,256]{1,0:T(8,128)(2,1)} %key_hbm.1, bf16[64,256]{1,0:T(8,128)(2,1)} %value_hbm.1), custom_call_target="tpu_custom_call" | custom-call | flops 20000000000 | bytes 1 | tf_op jit(solution)/shard_map/pack/pallas_call | solution.py:84
  2.2 22.9 %all_to_all.10.refs_2_.own_ref = bf16[16,24,640]{2,1,0:T(8,128)(2,1)S(1)} all-to-all(bf16[16,24,640]{2,1,0:T(8,128)(2,1)S(1)} %get-tuple-element.9), channel_id=1, replica_groups=mesh['ctx'=16,'tp'=2] {'ctx'}, dimensions={0} | all-to-all | bytes 983040 | tf_op jit(solution)/shard_map/all_to_all | solution.py:423
  25.1 0.0 collective-permute-start.5
  25.1 1.9 %collective-permute-done.5.rest_ref = bf16[16,24,640]{2,1,0:T(8,128)(2,1)S(1)} collective-permute-done((bf16[16,24,640]{2,1,0:T(8,128)(2,1)S(1)}, bf16[16,24,640]{2,1,0:T(8,128)(2,1)S(1)}, u32[]{:S(2)}, u32[]{:S(2)}) %collective-permute-start.5) | collective-permute-done | bytes 491552 | tf_op jit(solution)/shard_map/ppermute | solution.py:437
  26.9 0.0 copy-done
  26.9 0.0 copy-done.1
  26.9 7.8 %gate_up.1 = (bf16[96,2048]{1,0:T(8,128)(2,1)S(1)}, bf16[3584,2560]{1,0:T(8,128)(2,1)S(1)}) custom-call(s32[1]{0:T(128)} %bitcast.3.side_ref, bf16[16,24,640]{2,1,0:T(8,128)(2,1)S(1)} %all_to_all.10.refs_2_.own_ref, bf16[16,24,640]{2,1,0:T(8,128)(2,1)S(1)} %collective-permute-done.5.rest_ref, bf16[1,5120,2048]{2,1,0:T(8,128)(2,1)S(1)} %copy-done, ...), custom_call_target="tpu_custom_call" | custom-call | flops 4026531840 | bytes 10485760 | tf_op jit(solution)/shard_map/gate_up/pallas_call | solution.py:166
  34.7 0.2 collective-permute-start.6
  34.9 1.6 %collective-permute-done.6.rest_ref = bf16[96,2048]{1,0:T(8,128)(2,1)S(1)} collective-permute-done((bf16[96,2048]{1,0:T(8,128)(2,1)S(1)}, bf16[96,2048]{1,0:T(8,128)(2,1)S(1)}, u32[]{:S(2)}, u32[]{:S(2)}) %collective-permute-start.6) | collective-permute-done | bytes 393248 | tf_op jit(solution)/shard_map/ppermute | solution.py:439
  36.5 0.0 copy-start.2
  36.5 0.0 copy-start.3
  36.5 0.0 copy-start.4
  36.5 4.7 %down.1 = bf16[16,24,640]{2,1,0:T(8,128)(2,1)} custom-call(s32[1]{0:T(128)} %bitcast.3.side_ref, bf16[96,2048]{1,0:T(8,128)(2,1)S(1)} %get-tuple-element.12.own_ref, bf16[96,2048]{1,0:T(8,128)(2,1)S(1)} %collective-permute-done.6.rest_ref, bf16[3584,2560]{1,0:T(8,128)(2,1)S(1)} %get-tuple-element.13.wd_ref, bf16[1,4096,2560]{2,1,0:T(8,128)(2,1)} %wd_hbm.3), custom_call_target="tpu_custom_call" | custom-call | flops 2013265920 | bytes 10485760 | tf_op jit(solution)/shard_map/down/pallas_call | solution.py:253
  41.2 3.8 %all-to-all-start.1 = ((bf16[16,24,640]{2,1,0:T(8,128)(2,1)}), bf16[16,24,640]{2,1,0:T(8,128)(2,1)S(1)}, u32[]{:S(2)}, u32[]{:S(2)}) async-start(bf16[16,24,640]{2,1,0:T(8,128)(2,1)} %down.1), calls=%async_computation.1 | async-start | bytes 983040 | tf_op jit(solution)/shard_map/all_to_all | solution.py:441
  45.1 1.9 %collective-permute-start = (bf16[64,512]{1,0:T(8,128)(2,1)S(1)}, bf16[64,512]{1,0:T(8,128)(2,1)S(1)}, u32[]{:S(2)}, u32[]{:S(2)}) collective-permute-start(bf16[64,512]{1,0:T(8,128)(2,1)S(1)} %get-tuple-element.8.refs_0_), channel_id=1, source_target_pairs={{0,8},{2,10},{4,12},{6,14},{8,0},{10,2},{12,4},{14,6},{16,24},{18,... | collective-permute-start | bytes 196616 | tf_op jit(solution)/shard_map/ppermute | solution.py:422
  47.0 9.2 %collective-permute-done.refs_1_ = bf16[64,512]{1,0:T(8,128)(2,1)S(1)} collective-permute-done((bf16[64,512]{1,0:T(8,128)(2,1)S(1)}, bf16[64,512]{1,0:T(8,128)(2,1)S(1)}, u32[]{:S(2)}, u32[]{:S(2)}) %collective-permute-start) | collective-permute-done | bytes 65568 | tf_op jit(solution)/shard_map/ppermute | solution.py:422
  56.3 5.0 %collective-permute-start.1 = (bf16[128,512]{1,0:T(8,128)(2,1)S(1)}, bf16[128,512]{1,0:T(8,128)(2,1)S(1)}, u32[]{:S(2)}, u32[]{:S(2)}) collective-permute-start(bf16[128,512]{1,0:T(8,128)(2,1)S(1)} %join.2.refs_0_), channel_id=1, source_target_pairs={{0,16},{2,18},{4,20},{6,22},{8,24},{10,26},{12,28},{14,30},{1,17},... | collective-permute-start | bytes 393224 | tf_op jit(solution)/shard_map/ppermute | solution.py:425
  61.3 2.5 %collective-permute-done.1.refs_1_ = bf16[128,512]{1,0:T(8,128)(2,1)S(1)} collective-permute-done((bf16[128,512]{1,0:T(8,128)(2,1)S(1)}, bf16[128,512]{1,0:T(8,128)(2,1)S(1)}, u32[]{:S(2)}, u32[]{:S(2)}) %collective-permute-start.1) | collective-permute-done | bytes 131104 | tf_op jit(solution)/shard_map/ppermute | solution.py:425
  63.8 2.4 %collective-permute-start.4 = (bf16[256,512]{1,0:T(8,128)(2,1)S(1)}, bf16[256,512]{1,0:T(8,128)(2,1)S(1)}, u32[]{:S(2)}, u32[]{:S(2)}) collective-permute-start(bf16[256,512]{1,0:T(8,128)(2,1)S(1)} %join.3.refs_0_), channel_id=1, source_target_pairs={{0,6},{2,4},{4,2},{6,0},{8,14},{10,12},{12,10},{14,8},{16,22},{18,... | collective-permute-start | bytes 786440 | tf_op jit(solution)/shard_map/ppermute | solution.py:429
  66.2 0.6 collective-permute-start.3
  66.8 0.6 collective-permute-start.2
  67.4 6.6 %collective-permute-done.4.refs_3_ = bf16[256,512]{1,0:T(8,128)(2,1)S(1)} collective-permute-done((bf16[256,512]{1,0:T(8,128)(2,1)S(1)}, bf16[256,512]{1,0:T(8,128)(2,1)S(1)}, u32[]{:S(2)}, u32[]{:S(2)}) %collective-permute-start.4) | collective-permute-done | bytes 262176 | tf_op jit(solution)/shard_map/ppermute | solution.py:429
  74.0 2.8 %collective-permute-done.3.refs_2_ = bf16[256,512]{1,0:T(8,128)(2,1)S(1)} collective-permute-done((bf16[256,512]{1,0:T(8,128)(2,1)S(1)}, bf16[256,512]{1,0:T(8,128)(2,1)S(1)}, u32[]{:S(2)}, u32[]{:S(2)}) %collective-permute-start.3) | collective-permute-done | bytes 262176 | tf_op jit(solution)/shard_map/ppermute | solution.py:429
  76.8 0.0 collective-permute-done.2.refs_1_
  76.8 0.0 copy-done.2
  76.8 0.0 copy-done.3
  76.8 0.0 copy-done.4
  76.8 2.1 %attend.1 = (bf16[64,1280]{1,0:T(8,128)(2,1)}, f32[64,256]{1,0:T(8,128)S(1)}) custom-call(s32[1]{0:T(128)} %bitcast.place_ref, s32[1,64]{1,0:T(1,128)S(1)} %bitcast.5, f32[1,64]{1,0:T(1,128)S(1)} %bitcast.6, bf16[64,1280]{1,0:T(8,128)(2,1)S(1)} %copy-done.2, bf16[256,512]{1,0:T(8,128)(2,1)S(1)} %join.3.refs_0_, ...), custom_call_target="tpu_custom_call" | custom-call | tf_op jit(solution)/shard_map/attend/pallas_call | solution.py:395
  78.9 0.0 all-to-all-done.1.back_ref
  78.9 1.2 %combine.1 = bf16[64,2560]{1,0:T(8,128)(2,1)} custom-call(f32[64,256]{1,0:T(8,128)S(1)} %get-tuple-element.11.route_ref, bf16[16,24,640]{2,1,0:T(8,128)(2,1)S(1)} %all-to-all-done.1.back_ref), custom_call_target="tpu_custom_call" | custom-call | tf_op jit(solution)/shard_map/combine/pallas_call | solution.py:304
  (2 shorter events, 0.0 us)
Async XLA Ops:
  0.6 26.3 %copy-start = (bf16[1,5120,2048]{2,1,0:T(8,128)(2,1)S(1)}, bf16[1,5120,2048]{2,1,0:T(8,128)(2,1)}, u32[]{:S(2)}) copy-start(bf16[1,5120,2048]{2,1,0:T(8,128)(2,1)} %wg_ref.1) | copy-start | bytes 62914564
  0.6 26.3 %copy-start.1 = (bf16[1,5120,2048]{2,1,0:T(8,128)(2,1)S(1)}, bf16[1,5120,2048]{2,1,0:T(8,128)(2,1)}, u32[]{:S(2)}) copy-start(bf16[1,5120,2048]{2,1,0:T(8,128)(2,1)} %wu_ref.1) | copy-start | bytes 62914564
  25.1 1.9 %collective-permute-start.5 = (bf16[16,24,640]{2,1,0:T(8,128)(2,1)S(1)}, bf16[16,24,640]{2,1,0:T(8,128)(2,1)S(1)}, u32[]{:S(2)}, u32[]{:S(2)}) collective-permute-start(bf16[16,24,640]{2,1,0:T(8,128)(2,1)S(1)} %all_to_all.10.refs_2_.own_ref), channel_id=1, source_target_pairs={{0,1},{1,0},{2,3},{3,2},{4,5},{5,4},{6,7},{7,6},{8,9},{9,8},{10,11... | collective-permute-start | bytes 1474568 | tf_op jit(solution)/shard_map/ppermute | solution.py:437
  34.7 1.8 %collective-permute-start.6 = (bf16[96,2048]{1,0:T(8,128)(2,1)S(1)}, bf16[96,2048]{1,0:T(8,128)(2,1)S(1)}, u32[]{:S(2)}, u32[]{:S(2)}) collective-permute-start(bf16[96,2048]{1,0:T(8,128)(2,1)S(1)} %get-tuple-element.12.own_ref), channel_id=1, source_target_pairs={{0,1},{1,0},{2,3},{3,2},{4,5},{5,4},{6,7},{7,6},{8,9},{9,8},{10,11... | collective-permute-start | bytes 1179656 | tf_op jit(solution)/shard_map/ppermute | solution.py:439
  36.5 40.3 %copy-start.2 = (bf16[64,1280]{1,0:T(8,128)(2,1)S(1)}, bf16[64,1280]{1,0:T(8,128)(2,1)}, u32[]{:S(2)}) copy-start(bf16[64,1280]{1,0:T(8,128)(2,1)} %query_ref.1) | copy-start | bytes 491524
  36.5 40.3 %copy-start.3 = (s32[64,1]{0,1:T(1,128)S(1)}, s32[64,1]{0,1:T(1,128)}, u32[]{:S(2)}) copy-start(s32[64,1]{0,1:T(1,128)} %param.13) | copy-start | bytes 772
  36.5 40.3 %copy-start.4 = (f32[64]{0:T(128)S(1)}, f32[64]{0:T(128)}, u32[]{:S(2)}) copy-start(f32[64]{0:T(128)} %param.14) | copy-start | bytes 772
  41.2 37.7 %all-to-all-start.1 = ((bf16[16,24,640]{2,1,0:T(8,128)(2,1)}), bf16[16,24,640]{2,1,0:T(8,128)(2,1)S(1)}, u32[]{:S(2)}, u32[]{:S(2)}) async-start(bf16[16,24,640]{2,1,0:T(8,128)(2,1)} %down.1), calls=%async_computation.1 | async-start | bytes 983040 | tf_op jit(solution)/shard_map/all_to_all | solution.py:441
  45.1 11.2 %collective-permute-start = (bf16[64,512]{1,0:T(8,128)(2,1)S(1)}, bf16[64,512]{1,0:T(8,128)(2,1)S(1)}, u32[]{:S(2)}, u32[]{:S(2)}) collective-permute-start(bf16[64,512]{1,0:T(8,128)(2,1)S(1)} %get-tuple-element.8.refs_0_), channel_id=1, source_target_pairs={{0,8},{2,10},{4,12},{6,14},{8,0},{10,2},{12,4},{14,6},{16,24},{18,... | collective-permute-start | bytes 196616 | tf_op jit(solution)/shard_map/ppermute | solution.py:422
  56.3 7.5 %collective-permute-start.1 = (bf16[128,512]{1,0:T(8,128)(2,1)S(1)}, bf16[128,512]{1,0:T(8,128)(2,1)S(1)}, u32[]{:S(2)}, u32[]{:S(2)}) collective-permute-start(bf16[128,512]{1,0:T(8,128)(2,1)S(1)} %join.2.refs_0_), channel_id=1, source_target_pairs={{0,16},{2,18},{4,20},{6,22},{8,24},{10,26},{12,28},{14,30},{1,17},... | collective-permute-start | bytes 393224 | tf_op jit(solution)/shard_map/ppermute | solution.py:425
  63.8 10.2 %collective-permute-start.4 = (bf16[256,512]{1,0:T(8,128)(2,1)S(1)}, bf16[256,512]{1,0:T(8,128)(2,1)S(1)}, u32[]{:S(2)}, u32[]{:S(2)}) collective-permute-start(bf16[256,512]{1,0:T(8,128)(2,1)S(1)} %join.3.refs_0_), channel_id=1, source_target_pairs={{0,6},{2,4},{4,2},{6,0},{8,14},{10,12},{12,10},{14,8},{16,22},{18,... | collective-permute-start | bytes 786440 | tf_op jit(solution)/shard_map/ppermute | solution.py:429
  66.2 10.6 %collective-permute-start.3 = (bf16[256,512]{1,0:T(8,128)(2,1)S(1)}, bf16[256,512]{1,0:T(8,128)(2,1)S(1)}, u32[]{:S(2)}, u32[]{:S(2)}) collective-permute-start(bf16[256,512]{1,0:T(8,128)(2,1)S(1)} %join.3.refs_0_), channel_id=1, source_target_pairs={{0,4},{2,6},{4,0},{6,2},{8,12},{10,14},{12,8},{14,10},{16,20},{18,... | collective-permute-start | bytes 786440 | tf_op jit(solution)/shard_map/ppermute | solution.py:429
  66.8 10.0 %collective-permute-start.2 = (bf16[256,512]{1,0:T(8,128)(2,1)S(1)}, bf16[256,512]{1,0:T(8,128)(2,1)S(1)}, u32[]{:S(2)}, u32[]{:S(2)}) collective-permute-start(bf16[256,512]{1,0:T(8,128)(2,1)S(1)} %join.3.refs_0_), channel_id=1, source_target_pairs={{0,2},{2,0},{4,6},{6,4},{8,10},{10,8},{12,14},{14,12},{16,18},{18,... | collective-permute-start | bytes 786440 | tf_op jit(solution)/shard_map/ppermute | solution.py:429
